TPU v7x, 512 devices: a 4x2x32 block of a 4x8x32 slice. The times are simulated.
512 devices in a mesh: groups: 2 (over y), tp: 64 (over z, core), seq: 4 (over x).
Axes of the slice: x: 4, y: 2, z: 32, core: 2. Of those that a mesh axis runs over, the one named last changes fastest.
The devices are a block of a 4x8x32 slice.
Arguments:
- kv_prefill: bfloat16 [2, 2, 8, 32768, 128], P(None, None, 'groups', ('tp', 'seq')), parts along dimension 2, may hold values from -10 to 10
- queries: bfloat16 [2, 8, 64, 128], P(None, ('groups', 'seq'), 'tp'), parts along dimension 1, may hold values from -512 to 512
- new_kv: bfloat16 [2, 2, 8, 8, 128], P(None, None, ('groups', 'seq')), parts along dimension 2, may hold values from -4.5 to 4.5
- lengths: int32 [8], P(('groups', 'seq')), parts along dimension 0, may hold values from 2048 to 4095
- page_slots: int32 [8, 256], P(('groups', 'seq')), parts along dimension 0, may hold values from 0 to 255, each once within a row
Outputs:
- decode_pool: bfloat16 [2, 2, 64, 2048, 16, 128], P(None, None, 'tp', ('groups', 'seq')), parts along dimension 3
- attention_out: bfloat16 [2, 8, 64, 128], P(None, ('groups', 'seq'), 'tp'), parts along dimension 1
There are 2 independent parts, one for each index of `groups`. A program takes and returns all parts, laid end to end along the dimension named above; each array names one. Nothing has to cross between parts.
Inputs may be any that keep to these rules, and one draw needn't show every extreme that they name: Row b belongs to sequence b: its page j goes to slot page_slots[b, j] of the row's block of 256 slots; each row uses every slot once.
All inputs are finite; a program needn't handle non-finite values.
Results may differ from a plain program's by a relative error of at most 0.01.
Values may be sent and summed in bfloat16 or wider, within the bound.
A program may use at most 64 MiB of HBM per device.

v0:
```python
import math

import jax
import jax.numpy as jnp
from jax import lax
from jax.sharding import PartitionSpec as P

KVH = 8
PAGE = 16
CTX = 4096


def swapped(array, axis, bit):
    return lax.ppermute(array, axis, [(i, i ^ 1 << bit) for i in range(lax.axis_size(axis))])


def spread_heads(blocks, axis_dim):
    tp_ranks = lax.axis_size("tp")
    kv_rank = max(1, KVH // tp_ranks)
    fanout = tp_ranks * kv_rank // KVH
    levels = fanout.bit_length() - 1
    ordering = list(range(levels - 1, -1, -1))
    my_rank = lax.axis_index("tp")
    finished = []
    for bit_index in ordering:
        partner = swapped(blocks, "tp", bit_index)
        lower_side = my_rank // (1 << bit_index) % 2 == 0
        lower_part = jnp.where(lower_side, blocks, partner)
        upper_part = jnp.where(lower_side, partner, blocks)
        higher_bits = sum((1 for earlier in finished if earlier > bit_index))
        shape_now = blocks.shape
        outer_count = 2**higher_bits
        split_shape = (
            shape_now[:axis_dim]
            + (outer_count, shape_now[axis_dim] // outer_count)
            + shape_now[axis_dim + 1 :]
        )
        paired = jnp.stack(
            (lower_part.reshape(split_shape), upper_part.reshape(split_shape)), axis=axis_dim + 1
        )
        blocks = paired.reshape(
            shape_now[:axis_dim] + (2 * shape_now[axis_dim],) + shape_now[axis_dim + 1 :]
        )
        finished.append(bit_index)
    return blocks


def repack(grouped, page_row, local_seqs):
    layers_here = grouped.shape[1]
    head_count = grouped.shape[3] // CTX
    head_dim = grouped.shape[4]
    paged_rows = grouped.reshape(
        2, layers_here, local_seqs, head_count, CTX // PAGE, PAGE, head_dim
    )
    paged_rows = paged_rows.transpose(0, 1, 3, 2, 4, 5, 6).reshape(
        2, layers_here, head_count, local_seqs * (CTX // PAGE), PAGE, head_dim
    )
    inverse = jnp.argsort(page_row)
    return jnp.take(paged_rows, inverse, axis=3)


def body(kv_prefill, queries, new_kv, lengths, page_slots):
    local_seqs = lengths.shape[0]
    page_row = page_slots[0]
    tp_ranks = lax.axis_size("tp")
    kv_rank = max(1, KVH // tp_ranks)
    layer_count = kv_prefill.shape[1]
    decode_pool = repack(
        spread_heads(lax.all_to_all(kv_prefill, "seq", split_axis=2, concat_axis=3, tiled=True), 3),
        page_row,
        local_seqs,
    )
    first_head = lax.axis_index("tp") * KVH // tp_ranks
    fresh_rows = lax.dynamic_slice_in_dim(new_kv, first_head, kv_rank, 3)
    pages_per = CTX // PAGE
    length_now = lengths[0]
    slot_now = lax.dynamic_index_in_dim(page_row, 0 + length_now // PAGE, 0, False)
    update = fresh_rows[:, :, 0][:, :, :, None, None, :]
    decode_pool = lax.dynamic_update_slice(
        decode_pool, update, (0, 0, 0, slot_now, length_now % PAGE, 0)
    )
    slot_table = page_row.reshape(local_seqs, pages_per)
    head_dim = queries.shape[3]
    key_cache = jnp.take(decode_pool[0], slot_table, axis=2).reshape(
        layer_count, kv_rank, local_seqs, CTX, head_dim
    )
    values = jnp.take(decode_pool[1], slot_table, axis=2).reshape(
        layer_count, kv_rank, local_seqs, CTX, head_dim
    )
    grouped_q = queries.reshape(
        layer_count, local_seqs, kv_rank, queries.shape[2] // kv_rank, head_dim
    )
    scores = jnp.einsum(
        "lskgd,lkstd->lskgt", grouped_q, key_cache, preferred_element_type=jnp.float32
    ) * (1.0 / math.sqrt(head_dim))
    positions = jnp.arange(CTX, dtype=jnp.int32)
    visible = (positions[None, :] <= lengths[:, None])[None, :, None, None, :]
    masked = jnp.where(visible, scores, -1e30)
    highest = jnp.max(masked, axis=-1, keepdims=True)
    exponent = jnp.where(visible, jnp.exp(masked - highest), 0.0)
    weights = (exponent / jnp.sum(exponent, axis=-1, keepdims=True)).astype(jnp.bfloat16)
    mixed_out = jnp.einsum(
        "lskgt,lkstd->lskgd", weights, values, preferred_element_type=jnp.float32
    )
    attention_out = mixed_out.astype(jnp.bfloat16).reshape(queries.shape)
    return (decode_pool, attention_out)


def solution(mesh):
    placed = (
        P(None, None, "groups", ("tp", "seq"), None),
        P(None, ("groups", "seq"), "tp", None),
        P(None, None, ("groups", "seq"), None, None),
        P(("groups", "seq")),
        P(("groups", "seq"), None),
    )
    return jax.shard_map(
        body,
        mesh=mesh,
        in_specs=placed,
        out_specs=(
            P(None, None, "tp", ("groups", "seq"), None, None),
            P(None, ("groups", "seq"), "tp", None),
        ),
        check_vma=False,
    )
```

profile of v0, /device:TPU:33, one launch (start us, length us, event | category | flops | bytes accessed | tf_op | source)
XLA Modules:
  0.0 126.1 jit_solution(5316480611457017284)
XLA Ops:
  0.6 0.0 copy-start
  0.6 1.1 copy.29
  1.7 11.9 %all_to_all.12 = bf16[2,2,4,128,128]{4,3,1,0,2:T(8,128)(2,1)S(1)} all-to-all(bf16[2,2,4,128,128]{4,3,1,0,2:T(8,128)(2,1)S(1)} %copy.29), channel_id=1, replica_groups=mesh['groups'=2,'tp'=64,'seq'=4] {'seq'}, dimensions={2} | all-to-all | bytes 1048576 | tf_op jit(solution)/shard_map/all_to_all | solution.py:69
  13.6 8.3 %collective-permute-start = (bf16[2,2,1,512,128]{4,3,1,0,2:T(8,128)(2,1)S(1)}, bf16[2,2,1,512,128]{4,3,1,0,2:T(8,128)(2,1)S(1)}, u32[]{:S(2)}, u32[]{:S(2)}) collective-permute-start(bf16[2,2,1,512,128]{4,3,1,0,2:T(8,128)(2,1)S(1)} %bitcast.90), channel_id=1, source_target_pairs={{0,16},{4,20},{8,24},{12,28},{16,0},{20,4},{24,8},{28,12},{32,48},... | collective-permute-start | bytes 1572872 | tf_op jit(solution)/shard_map/ppermute | solution.py:14
  22.0 17.8 %collective-permute-done = bf16[2,2,1,512,128]{4,3,1,0,2:T(8,128)(2,1)S(1)} collective-permute-done((bf16[2,2,1,512,128]{4,3,1,0,2:T(8,128)(2,1)S(1)}, bf16[2,2,1,512,128]{4,3,1,0,2:T(8,128)(2,1)S(1)}, u32[]{:S(2)}, u32[]{:S(2)}) %collective-permute-start) | collective-permute-done | bytes 524320 | tf_op jit(solution)/shard_map/ppermute | solution.py:14
  39.7 0.2 select_bitcast_fusion.1
  39.9 0.1 pad_maximum_fusion.2
  40.0 2.6 %collective-permute-start.1 = (bf16[2,2,1,1024,128]{4,3,1,0,2:T(8,128)(2,1)S(1)}, bf16[2,2,1,1024,128]{4,3,1,0,2:T(8,128)(2,1)S(1)}, u32[]{:S(2)}, u32[]{:S(2)}) collective-permute-start(bf16[2,2,1,1024,128]{4,3,1,0,2:T(8,128)(2,1)S(1)} %bitcast.86), channel_id=1, source_target_pairs={{0,8},{4,12},{8,0},{12,4},{16,24},{20,28},{24,16},{28,20},{32,40},... | collective-permute-start | bytes 3145736 | tf_op jit(solution)/shard_map/ppermute | solution.py:14
  42.6 13.0 %collective-permute-done.1 = bf16[2,2,1,1024,128]{4,3,1,0,2:T(8,128)(2,1)S(1)} collective-permute-done((bf16[2,2,1,1024,128]{4,3,1,0,2:T(8,128)(2,1)S(1)}, bf16[2,2,1,1024,128]{4,3,1,0,2:T(8,128)(2,1)S(1)}, u32[]{:S(2)}, u32[]{:S(2)}) %collective-permute-start.1) | collective-permute-done | bytes 1048608 | tf_op jit(solution)/shard_map/ppermute | solution.py:14
  55.6 0.1 broadcast_select_fusion.3
  55.7 0.0 copy-start.2
  55.7 0.2 pad_maximum_fusion.1
  55.9 29.1 %collective-permute-start.2 = (bf16[2,2,1,2048,128]{4,3,1,0,2:T(8,128)(2,1)S(1)}, bf16[2,2,1,2048,128]{4,3,1,0,2:T(8,128)(2,1)}, u32[]{:S(2)}, u32[]{:S(2)}) collective-permute-start(bf16[2,2,1,2048,128]{4,3,1,0,2:T(8,128)(2,1)S(1)} %bitcast.83), channel_id=1, source_target_pairs={{0,4},{4,0},{8,12},{12,8},{16,20},{20,16},{24,28},{28,24},{32,36},... | collective-permute-start | bytes 6291464 | tf_op jit(solution)/shard_map/ppermute | solution.py:14
  85.7 0.0 copy-done.2
  85.7 0.6 constant_dynamic-slice_fusion
  87.6 3.2 %sort.17 = (s32[256]{0:T(256)}, s32[256]{0:T(256)S(1)}) sort(s32[256]{0:T(256)S(1)} %bitcast.92, s32[256]{0:T(256)S(1)} %iota.10), dimensions={0}, to_apply=%region_0.1 | sort | flops 2048 | bytes 4096 | tf_op jit(solution)/shard_map/jit(argsort)/sort | solution.py:58
  91.4 0.0 copy-done
  91.5 0.0 collective-permute-done.2
  91.5 1.9 %broadcast_select_fusion.1 = (bf16[2,2,1,2048,128]{4,3,1,0,2:T(8,128)(2,1)S(1)}, bf16[2,2,1,2048,128]{4,3,1,0,2:T(8,128)(2,1)S(1)}) fusion(bf16[2,2,1,2048,128]{4,3,1,0,2:T(8,128)(2,1)} %collective-permute-done.2, pred[]{:T(512)S(6)} %eq.14, bf16[2,2,1,2,2,512,128]{6,5,4,3,1,0,2:T(8,128)(2,1)S(1)} %pad_maximum_fusion.1), kind=kLoop, calls=%fused_computation.11 | loop fusion | flops 2097152 | bytes 8388609 | tf_op jit(solution)/shard_map/jit(_where)/select_n | solution.py:28
  93.4 2.4 %pad_maximum_fusion = bf16[2,2,1,4,2,512,128]{6,5,4,3,1,0,2:T(8,128)(2,1)} fusion(bf16[2,2,1,4,1,512,128]{6,5,4,3,1,0,2:T(8,128)(2,1)S(1)} %bitcast.85, bf16[2,2,1,4,1,512,128]{6,5,4,3,1,0,2:T(8,128)(2,1)S(1)} %bitcast.84), kind=kLoop, calls=%fused_computation.3 | loop fusion | flops 2097152 | bytes 8388608 | tf_op jit(solution)/shard_map/stack | solution.py:38
  95.8 5.5 %gather_fusion = bf16[256,2,2,16,128]{4,3,2,1,0:T(8,128)(2,1)} fusion(bf16[2,2,256,16,128]{4,3,2,1,0:T(8,128)(2,1)} %bitcast.80, s32[1024]{0:T(1024)S(1)} %pad_clamp_fusion.1), kind=kCustom, calls=%fused_computation.2 | custom fusion | bytes 8389632 | tf_op jit(solution)/shard_map/jit(_take)/gather | solution.py:59
  101.2 4.0 %bitcast_select_fusion = bf16[2,2,1,256,16,128]{5,4,1,0,3,2:T(8,128)(2,1)} fusion(bf16[256,2,2,16,128]{4,3,2,1,0:T(8,128)(2,1)} %gather_fusion, pred[256]{0:T(512)(128)(4,1)S(1)} %compare_and_fusion), kind=kLoop, calls=%fused_computation.4 | loop fusion | flops 2097152 | bytes 8388864 | tf_op jit(solution)/shard_map/jit(_take)/select_n | solution.py:59
  105.3 1.3 %dynamic_update_slice.3 = bf16[2,2,1,256,16,128]{5,4,1,0,3,2:T(8,128)(2,1)} dynamic-update-slice(bf16[2,2,1,256,16,128]{5,4,1,0,3,2:T(8,128)(2,1)} %bitcast_select_fusion, bf16[2,2,1,1,1,128]{5,4,1,0,3,2:T(2,128)(2,1)S(1)} %dynamic-slice_bitcast_fusion, s32[]{:T(128)} %constant.109.clone.1, s32[]{:T(128)} %constant.109.clone.1, s32[]{:T(128)} %constant.109.clone.1, s32[]{:T(128)S(6)} %select_n.143, ...) | dynamic-update-slice | bytes 2052 | tf_op jit(solution)/shard_map/dynamic_update_slice | solution.py:79
  106.6 0.0 copy-start.1
  106.6 5.1 %slice_bitcast_fusion.1 = (bf16[2,256,16,128]{3,2,0,1:T(8,128)(2,1)}, bf16[2,256,16,128]{3,2,0,1:T(8,128)(2,1)}) fusion(bf16[2,2,1,256,16,128]{5,4,1,0,3,2:T(8,128)(2,1)} %dynamic_update_slice.3), kind=kLoop, calls=%fused_computation.6 | loop fusion | bytes 8388608 | tf_op jit(solution)/shard_map/jit(_take)/Arg_0.23 | solution.py:84
  111.7 0.0 copy-done.1
  111.7 2.7 %copy.38 = bf16[2,2,1,256,16,128]{5,4,3,2,1,0:T(8,128)(2,1)} copy(bf16[2,2,1,256,16,128]{5,4,1,0,3,2:T(8,128)(2,1)S(1)} %copy-done.1) | data formatting | bytes 8388608
  114.5 2.6 %gather_fusion.1 = bf16[256,2,16,128]{3,2,1,0:T(8,128)(2,1)S(1)} fusion(bf16[2,256,16,128]{3,2,0,1:T(8,128)(2,1)} %get-tuple-element.17, s32[1024]{0:T(1024)S(1)} %pad_clamp_fusion), kind=kCustom, calls=%fused_computation.clone | custom fusion | bytes 4195328 | tf_op jit(solution)/shard_map/jit(_take)/gather | solution.py:84
  117.1 3.7 %gather_fusion.2 = bf16[256,2,16,128]{3,2,1,0:T(8,128)(2,1)} fusion(bf16[2,256,16,128]{3,2,0,1:T(8,128)(2,1)} %get-tuple-element.18, s32[1024]{0:T(1024)S(1)} %pad_clamp_fusion), kind=kCustom, calls=%fused_computation.1.clone | custom fusion | bytes 4195328 | tf_op jit(solution)/shard_map/jit(_take)/gather | solution.py:87
  120.8 2.2 %bitcast_select_fusion.2 = (bf16[2,1,1,256,16,128]{5,4,0,3,2,1:T(8,128)(2,1)S(1)}, bf16[2,1,1,256,16,128]{5,4,0,3,2,1:T(8,128)(2,1)S(1)}) fusion(bf16[256,2,16,128]{3,2,1,0:T(8,128)(2,1)S(1)} %gather_fusion.1, pred[256]{0:T(512)(128)(4,1)S(1)} %get-tuple-element.15, bf16[256,2,16,128]{3,2,1,0:T(8,128)(2,1)} %gather_fusion.2), kind=kLoop, calls=%fused_computation.9 | loop fusion | flops 2097152 | bytes 8388864 | tf_op jit(solution)/shard_map/jit(_take)/select_n | solution.py:84
  123.0 0.0 copy-start.3
  123.0 0.4 copy.36
  123.4 0.3 copy-done.3
  123.7 0.6 fusion.5
  124.3 0.2 fusion.4
  124.5 0.2 fusion.7
  124.7 0.4 copy.37
  125.1 0.1 fusion.3
  125.2 0.4 fusion.1
  125.6 0.5 convert_bitcast_fusion
  (9 shorter events, 0.1 us)
Async XLA Ops:
  0.6 90.8 %copy-start = (bf16[2,2,1,8,128]{4,3,2,1,0:T(8,128)(2,1)S(1)}, bf16[2,2,1,8,128]{4,3,2,1,0:T(8,128)(2,1)}, u32[]{:S(2)}) copy-start(bf16[2,2,1,8,128]{4,3,2,1,0:T(8,128)(2,1)} %param.9) | copy-start | bytes 24580
  13.6 26.1 %collective-permute-start = (bf16[2,2,1,512,128]{4,3,1,0,2:T(8,128)(2,1)S(1)}, bf16[2,2,1,512,128]{4,3,1,0,2:T(8,128)(2,1)S(1)}, u32[]{:S(2)}, u32[]{:S(2)}) collective-permute-start(bf16[2,2,1,512,128]{4,3,1,0,2:T(8,128)(2,1)S(1)} %bitcast.90), channel_id=1, source_target_pairs={{0,16},{4,20},{8,24},{12,28},{16,0},{20,4},{24,8},{28,12},{32,48},... | collective-permute-start | bytes 1572872 | tf_op jit(solution)/shard_map/ppermute | solution.py:14
  40.0 15.6 %collective-permute-start.1 = (bf16[2,2,1,1024,128]{4,3,1,0,2:T(8,128)(2,1)S(1)}, bf16[2,2,1,1024,128]{4,3,1,0,2:T(8,128)(2,1)S(1)}, u32[]{:S(2)}, u32[]{:S(2)}) collective-permute-start(bf16[2,2,1,1024,128]{4,3,1,0,2:T(8,128)(2,1)S(1)} %bitcast.86), channel_id=1, source_target_pairs={{0,8},{4,12},{8,0},{12,4},{16,24},{20,28},{24,16},{28,20},{32,40},... | collective-permute-start | bytes 3145736 | tf_op jit(solution)/shard_map/ppermute | solution.py:14
  55.7 30.0 %copy-start.2 = (s32[1,256]{1,0:T(1,128)S(1)}, s32[1,256]{1,0:T(1,128)}, u32[]{:S(2)}) copy-start(s32[1,256]{1,0:T(1,128)} %param.11) | copy-start | bytes 3076
  55.9 35.6 %collective-permute-start.2 = (bf16[2,2,1,2048,128]{4,3,1,0,2:T(8,128)(2,1)S(1)}, bf16[2,2,1,2048,128]{4,3,1,0,2:T(8,128)(2,1)}, u32[]{:S(2)}, u32[]{:S(2)}) collective-permute-start(bf16[2,2,1,2048,128]{4,3,1,0,2:T(8,128)(2,1)S(1)} %bitcast.83), channel_id=1, source_target_pairs={{0,4},{4,0},{8,12},{12,8},{16,20},{20,16},{24,28},{28,24},{32,36},... | collective-permute-start | bytes 6291464 | tf_op jit(solution)/shard_map/ppermute | solution.py:14
  106.6 5.1 %copy-start.1 = (bf16[2,2,1,256,16,128]{5,4,1,0,3,2:T(8,128)(2,1)S(1)}, bf16[2,2,1,256,16,128]{5,4,1,0,3,2:T(8,128)(2,1)}, u32[]{:S(2)}) copy-start(bf16[2,2,1,256,16,128]{5,4,1,0,3,2:T(8,128)(2,1)} %dynamic_update_slice.3) | copy-start | bytes 12582916
  123.0 0.7 copy-start.3
where the time goes:
time: 127 us; the launch traced here: 126 us
  starting transfers between devices  40 us (31%)
  waiting for transfers between devices  30.7 us (24%)
  local copies, waits for them, and re-layouts  23.7 us (19%)
  other arithmetic  15.3 us (12%)
  blocking collectives  11.9 us (9%)
  between operations  3.49 us (3%)
    ppermute x3, starting transfers between devices, swapped(): lax.ppermute(array, axis, [(i, i ^ 1 << bit) for i in range(lax.axis_size...  40 us
    ppermute x3, waiting for transfers between devices, swapped(): lax.ppermute(array, axis, [(i, i ^ 1 << bit) for i in range(lax.axis_size...  30.7 us
    all_to_all x1, blocking collectives, body(): lax.all_to_all(kv_prefill, 'seq', split_axis=2, concat_axis=3, tiled=True)  11.9 us
    gather x1, local copies, waits for them, and re-layouts, repack(): return jnp.take(paged_rows, inverse, axis=3)  5.46 us
    another operation x1, local copies, waits for them, and re-layouts, body(): jnp.take(decode_pool[0], slot_table, axis=2)  5.12 us
    unnamed x10, local copies, waits for them, and re-layouts  4.12 us
    select_n x2, other arithmetic, repack(): return jnp.take(paged_rows, inverse, axis=3)  4.05 us
    gather x1, local copies, waits for them, and re-layouts, body(): jnp.take(decode_pool[1], slot_table, axis=2)  3.74 us
  transfers between devices with their start and end apart: 3, of which 2 were waited for; matrix products, arithmetic and copies ran while one was open for 3% of the time, Pallas kernels for 0%

commit v1 on v0

v1 whole, which is shorter than its diff:
```python
import functools
import math

import jax
import jax.numpy as jnp
from jax import lax
from jax.experimental import pallas as pl
from jax.experimental.pallas import tpu as pltpu
from jax.sharding import PartitionSpec as P

KVH = 8
PAGE = 16
CTX = 4096
CORES = 2
MESH = pl.DeviceIdType.MESH
MIB = 1 << 20


def arrival_order(chips, kinds):
    order = []
    for _ in range(chips - 1):
        further = [(hops + 1, kind) for hops, kind in order]
        own = [(1, kind) for kind in kinds]
        order = own[:-1] + further[:1] + own[-1:] + further[1:]
    return order


def spread_kernel(kv, cache, own_sem, pair_sem, x_sent, up_sent, down_sent, pair_sent):
    tp, x = lax.axis_index("tp"), lax.axis_index("seq")
    ranks, nx = lax.axis_size("tp"), lax.axis_size("seq")
    fan = ranks // KVH
    chips = fan // CORES
    rank = lax.rem(tp, fan)
    z, core = rank // CORES, lax.rem(tp, CORES)
    pages = kv.shape[3]
    last = chips - 1
    up, down, pair = {"tp": tp + CORES}, {"tp": tp - CORES}, {"tp": tp + 1 - 2 * core}

    def seq_rank(steps):
        return lax.rem(x + steps + nx, nx)

    barrier = pltpu.get_barrier_semaphore()

    def greet(device):
        pl.semaphore_signal(barrier, inc=1, device_id=device, device_id_type=MESH)

    greet(pair)
    for step in range(1, nx):
        greet({"seq": seq_rank(step)})
    pl.when(z < last)(lambda: greet(up))
    pl.when(z > 0)(lambda: greet(down))
    pl.semaphore_wait(barrier, nx + jnp.where(z < last, 1, 0) + jnp.where(z > 0, 1, 0))

    def place(plane, kind, of_core):
        first = ((plane * CORES + of_core) * nx + seq_rank(kind)) * pages
        return cache.at[:, :, pl.ds(first, pages)]

    def remote(src, dst, sent, landed, device):
        return pltpu.make_async_remote_copy(
            src_ref=src, dst_ref=dst, send_sem=sent, recv_sem=landed, device_id=device, device_id_type=MESH
        )

    def along(plane, kind, sent, device, src=None):
        index = plane * nx + kind
        block = place(plane, kind, core)
        return remote(block if src is None else src, block, sent.at[index], own_sem.at[index], device)

    def to_pair(plane, kind, src=None):
        index = plane * nx + kind
        block = place(plane, kind, core)
        return remote(block if src is None else src, block, pair_sent.at[index], pair_sem.at[index], pair)

    def to_seq(kind):
        mine = ((z * CORES + core) * nx + x) * pages
        target = seq_rank(-kind)
        return remote(
            kv.at[:, :, target],
            cache.at[:, :, pl.ds(mine, pages)],
            x_sent.at[kind],
            own_sem.at[z * nx + kind],
            {"seq": target},
        )

    kinds = [0, *sorted(range(1, nx), key=lambda k: (min(k, nx - k), k))]
    mine = kv.at[:, :, x]
    pl.when(z > 0)(lambda: along(z, 0, down_sent, down, mine).start())
    pl.when(z < last)(lambda: along(z, 0, up_sent, up, mine).start())
    for kind in kinds[1:]:
        to_seq(kind).start()
    local = pltpu.make_async_copy(mine, place(z, 0, core), own_sem.at[z * nx])
    local.start()
    to_pair(z, 0, mine).start()

    def landed(plane, kind):
        along(plane, kind, up_sent, up).wait_recv()

    def own(kind):
        landed(z, kind)
        pl.when(z > 0)(lambda: along(z, kind, down_sent, down).start())
        pl.when(z < last)(lambda: along(z, kind, up_sent, up).start())
        to_pair(z, kind).start()

    def from_above(hops, kind):
        landed(z + hops, kind)
        pl.when(z > 0)(lambda: along(z + hops, kind, down_sent, down).start())
        to_pair(z + hops, kind).start()

    def from_below(hops, kind):
        landed(z - hops, kind)
        pl.when(z < last)(lambda: along(z - hops, kind, up_sent, up).start())
        to_pair(z - hops, kind).start()

    def passing(hops, kind):
        pl.when(z + hops <= last)(lambda: from_above(hops, kind))
        pl.when(z - hops >= 0)(lambda: from_below(hops, kind))

    order = arrival_order(chips, kinds)
    for kind in kinds[1:-1]:
        own(kind)
    passing(*order[0])
    own(kinds[-1])
    for hops, kind in order[1:]:
        passing(hops, kind)

    local.wait()
    for kind in kinds[1:]:
        to_seq(kind).wait_send()
    for plane in range(chips):
        for kind in kinds:
            to_pair(plane, kind).wait_send()
            partner_block = place(plane, kind, 1 - core)
            index = plane * nx + kind
            remote(partner_block, partner_block, pair_sent.at[index], pair_sem.at[index], pair).wait_recv()

            def sent_down(plane=plane, kind=kind):
                along(plane, kind, down_sent, down).wait_send()

            def sent_up(plane=plane, kind=kind):
                along(plane, kind, up_sent, up).wait_send()

            pl.when(jnp.logical_and(z > 0, plane >= z))(sent_down)
            pl.when(jnp.logical_and(z < last, plane <= z))(sent_up)


def attend(length, q, k, v, k_new, v_new):
    scale = 1.0 / math.sqrt(q.shape[1])
    contract = (((1,), (1,)), ((), ()))
    q8 = jnp.broadcast_to(q, (8, q.shape[1]))
    scores = lax.dot_general(q8, k, contract, preferred_element_type=jnp.float32) * scale
    t = lax.broadcasted_iota(jnp.int32, scores.shape, 1)
    scores = jnp.where(t < length, scores, -1e30)
    fresh = jnp.sum(q8.astype(jnp.float32) * k_new.astype(jnp.float32), axis=1, keepdims=True) * scale
    top = jnp.maximum(jnp.max(scores, axis=1, keepdims=True), fresh)
    weights = jnp.where(t < length, jnp.exp(scores - top), 0.0)
    fresh = jnp.exp(fresh - top)
    total = jnp.sum(weights, axis=1, keepdims=True) + fresh
    weights = (weights / total).astype(jnp.bfloat16)
    fresh = (fresh / total).astype(jnp.bfloat16).astype(jnp.float32)
    mixed = jnp.dot(weights, v, preferred_element_type=jnp.float32)
    mixed = mixed + fresh * v_new.astype(jnp.float32)
    return mixed[:1].astype(jnp.bfloat16)


def page_kernel(lengths, slots, cache, queries, new_kv, pool, out, staged, sem):
    layers, pages, head = cache.shape[1], cache.shape[2], cache.shape[4]
    length = lengths[0]
    slot_now, row_now = slots[0, length // PAGE], lax.rem(length, PAGE)
    head_now = lax.axis_index("tp") * KVH // lax.axis_size("tp")
    rows = lax.broadcasted_iota(jnp.int32, (PAGE, head), 0)

    def fresh(kind, layer):
        block = new_kv[kind, layer, 0].astype(jnp.float32)
        mine = lax.broadcasted_iota(jnp.int32, block.shape, 0) == head_now
        return jnp.sum(jnp.where(mine, block, 0.0), axis=0, keepdims=True).astype(jnp.bfloat16)

    copies = []
    for kind in range(2):
        for layer in range(layers):

            def move(page, _, kind=kind, layer=layer):
                staged[kind, layer, slots[0, page]] = cache[kind, layer, page]
                return 0

            lax.fori_loop(0, pages, move, 0, unroll=16)
            tile = staged[kind, layer, slot_now].astype(jnp.float32)
            tile = jnp.where(rows == row_now, fresh(kind, layer).astype(jnp.float32), tile)
            staged[kind, layer, slot_now] = tile.astype(jnp.bfloat16)
            copy = pltpu.make_async_copy(
                staged.at[kind, layer], pool.at[kind, layer, 0], sem.at[kind * layers + layer]
            )
            copy.start()
            copies.append(copy)

    for layer in range(layers):
        out[layer : layer + 1] = attend(
            length,
            queries[layer : layer + 1],
            cache[0, layer].reshape(CTX, head),
            cache[1, layer].reshape(CTX, head),
            fresh(0, layer),
            fresh(1, layer),
        )
    for copy in copies:
        copy.wait()


def body(kv_prefill, queries, new_kv, lengths, page_slots):
    kinds, layers, seqs, positions, head = kv_prefill.shape
    nx = lax.axis_size("seq")
    fan = lax.axis_size("tp") // KVH
    count = fan // CORES * nx
    pages = CTX // PAGE
    dma = pltpu.SemaphoreType.DMA
    anywhere = pl.BlockSpec(memory_space=pl.ANY)
    vmem = pl.BlockSpec(memory_space=pltpu.VMEM)
    smem = pl.BlockSpec(memory_space=pltpu.SMEM)
    cache_shape = (kinds, layers, pages, PAGE, head)
    cache = pl.pallas_call(
        spread_kernel,
        out_shape=pltpu.VMEM(cache_shape, kv_prefill.dtype),
        in_specs=[pl.BlockSpec(memory_space=pltpu.HBM)],
        out_specs=vmem,
        scratch_shapes=[dma((count,)), dma((count,)), dma((nx,)), dma((count,)), dma((count,)), dma((count,))],
        compiler_params=pltpu.CompilerParams(collective_id=0, has_side_effects=True, vmem_limit_bytes=16 * MIB),
        name="spread",
    )(kv_prefill.reshape(kinds, layers, seqs, positions // PAGE, PAGE, head))
    pool, out = pl.pallas_call(
        page_kernel,
        out_shape=(
            jax.ShapeDtypeStruct((kinds, layers, 1, pages, PAGE, head), kv_prefill.dtype),
            jax.ShapeDtypeStruct((layers, head), queries.dtype),
        ),
        in_specs=[smem, smem, vmem, vmem, vmem],
        out_specs=(anywhere, vmem),
        scratch_shapes=[pltpu.VMEM(cache_shape, kv_prefill.dtype), dma((kinds * layers,))],
        compiler_params=pltpu.CompilerParams(vmem_limit_bytes=24 * MIB),
        name="pages",
    )(lengths, page_slots, cache, queries.reshape(layers, head), new_kv)
    return pool, out.reshape(queries.shape)


def solution(mesh):
    placed = (
        P(None, None, "groups", ("tp", "seq"), None),
        P(None, ("groups", "seq"), "tp", None),
        P(None, None, ("groups", "seq"), None, None),
        P(("groups", "seq")),
        P(("groups", "seq"), None),
    )
    return jax.shard_map(
        body,
        mesh=mesh,
        in_specs=placed,
        out_specs=(
            P(None, None, "tp", ("groups", "seq"), None, None),
            P(None, ("groups", "seq"), "tp", None),
        ),
        check_vma=False,
    )
```

time: 127 us -> 83.2 us (0.66)
  Pallas kernels: 0 us -> 80.5 us
  starting transfers between devices: 40 us -> 0 us
  waiting for transfers between devices: 30.7 us -> 0 us
  local copies, waits for them, and re-layouts: 23.7 us -> 1.05 us
  other arithmetic: 15.3 us -> 0 us
  blocking collectives: 11.9 us -> 0 us
  between operations: 3.49 us -> 1.35 us
    pallas_call x0 -> x2, Pallas kernels: none -> 80.5 us  [the longest x1 75.6 us: body(): pl.pallas_call(spread_kernel, out_shape=pltpu.VMEM(cache_shape, kv_prefil...]
    ppermute x3 -> x0, starting transfers between devices: 40 us -> none  [swapped(): lax.ppermute(array, axis, [(i, i ^ 1 << bit) for i in range(lax.axis_size...]
    ppermute x3 -> x0, waiting for transfers between devices: 30.7 us -> none  [swapped(): lax.ppermute(array, axis, [(i, i ^ 1 << bit) for i in range(lax.axis_size...]
    all_to_all x1 -> x0, blocking collectives: 11.9 us -> none  [body(): lax.all_to_all(kv_prefill, 'seq', split_axis=2, concat_axis=3, tiled=True)]
    gather x3 -> x0, local copies, waits for them, and re-layouts: 11.8 us -> none  [the longest x1 5.46 us: repack(): return jnp.take(paged_rows, inverse, axis=3)]
    select_n x5 -> x0, other arithmetic: 8.27 us -> none  [the longest x2 4.05 us: repack(): return jnp.take(paged_rows, inverse, axis=3)]
    another operation x2 -> x0, local copies, waits for them, and re-layouts: 5.13 us -> none  [the longest x1 5.12 us: body(): jnp.take(decode_pool[0], slot_table, axis=2)]
    sort x1 -> x0, other arithmetic: 3.17 us -> none  [repack(): inverse = jnp.argsort(page_row)]
  transfers between devices with their start and end apart: 3 -> 0, of which waited for: 2 -> 0; matrix products, arithmetic and copies ran while one was open for 3% -> 0% of each run, Pallas kernels for 0% -> 0%
where the time goes in v1:
time: 83.2 us; the launch traced here: 82.9 us
  Pallas kernels  80.5 us (97%)
  between operations  1.35 us (2%)
  local copies, waits for them, and re-layouts  1.05 us (1%)
    pallas_call x1, Pallas kernels, body(): pl.pallas_call(spread_kernel, out_shape=pltpu.VMEM(cache_shape, kv_prefil...  75.6 us
    pallas_call x1, Pallas kernels, body(): pl.pallas_call(page_kernel, out_shape=(jax.ShapeDtypeStruct((kinds, layer...  4.93 us

profile of v1, /device:TPU:33, one launch (start us, length us, event | category | flops | bytes accessed | tf_op | source)
XLA Modules:
  0.0 82.9 jit_solution(12475664430053868630)
XLA Ops:
  0.6 0.0 copy-start.2
  0.6 0.0 copy-start.3
  1.3 0.0 copy-start
  1.3 1.0 %copy-done = bf16[2,2,4,128,128]{4,3,2,1,0:T(8,128)(2,1)S(1)} copy-done((bf16[2,2,4,128,128]{4,3,2,1,0:T(8,128)(2,1)S(1)}, bf16[2,2,4,128,128]{4,3,2,1,0:T(8,128)(2,1)}, u32[]{:S(2)}) %copy-start) | copy-done | bytes 524312
  2.4 0.0 copy-start.1
  2.4 75.6 %spread.1.cache = bf16[2,2,256,16,128]{4,3,2,1,0:T(8,128)(2,1)S(1)} custom-call(bf16[2,2,4,8,16,128]{5,4,3,2,1,0:T(8,128)(2,1)S(1)} %bitcast.3), custom_call_target="tpu_custom_call" | custom-call | tf_op jit(solution)/shard_map/spread/pallas_call | solution.py:218
  78.0 0.0 copy-done.2
  78.0 0.0 copy-done.3
  78.0 0.0 copy-done.1
  78.0 4.9 %pages.1 = (bf16[2,2,1,256,16,128]{5,4,3,2,1,0:T(8,128)(2,1)}, bf16[2,128]{1,0:T(2,128)(2,1)}) custom-call(s32[1]{0:T(128)S(6)} %copy.7.lengths, s32[1,256]{1,0:T(1,128)S(1)} %copy-done.2, bf16[2,2,256,16,128]{4,3,2,1,0:T(8,128)(2,1)S(1)} %spread.1.cache, bf16[2,128]{1,0:T(2,128)(2,1)S(1)} %bitcast.4, bf16[2,2,1,8,128]{4,3,2,1,0:T(8,128)(2,1)S(1)} %copy-done.1), custom_call_target="tpu_custom_call" | custom-call | tf_op jit(solution)/shard_map/pages/pallas_call | solution.py:227
Async XLA Ops:
  0.6 77.4 %copy-start.2 = (s32[1,256]{1,0:T(1,128)S(1)}, s32[1,256]{1,0:T(1,128)}, u32[]{:S(2)}) copy-start(s32[1,256]{1,0:T(1,128)} %slots.1) | copy-start | bytes 3076
  0.6 77.4 %copy-start.3 = (bf16[2,1,1,128]{3,0,2,1:T(2,128)(2,1)S(1)}, bf16[2,1,1,128]{3,0,2,1:T(2,128)(2,1)}, u32[]{:S(2)}) copy-start(bf16[2,1,1,128]{3,0,2,1:T(2,128)(2,1)} %param.6) | copy-start | bytes 1540
  1.3 1.0 %copy-start = (bf16[2,2,4,128,128]{4,3,2,1,0:T(8,128)(2,1)S(1)}, bf16[2,2,4,128,128]{4,3,2,1,0:T(8,128)(2,1)}, u32[]{:S(2)}) copy-start(bf16[2,2,4,128,128]{4,3,2,1,0:T(8,128)(2,1)} %param.5) | copy-start | bytes 1572868
  2.4 75.6 %copy-start.1 = (bf16[2,2,1,8,128]{4,3,2,1,0:T(8,128)(2,1)S(1)}, bf16[2,2,1,8,128]{4,3,2,1,0:T(8,128)(2,1)}, u32[]{:S(2)}) copy-start(bf16[2,2,1,8,128]{4,3,2,1,0:T(8,128)(2,1)} %new_kv.1) | copy-start | bytes 24580

commit v2 on v1

--- a/solution.py
+++ b/solution.py
@@ -25,7 +25,9 @@
     return order
 
 
-def spread_kernel(kv, cache, own_sem, pair_sem, x_sent, up_sent, down_sent, pair_sent):
+def spread_kernel(
+    kv, cache, own_sem, pair_sem, x_sent, up_sent, down_sent, pair_sent, local_sem, up_here, first_here
+):
     tp, x = lax.axis_index("tp"), lax.axis_index("seq")
     ranks, nx = lax.axis_size("tp"), lax.axis_size("seq")
     fan = ranks // KVH
@@ -34,112 +36,196 @@
     z, core = rank // CORES, lax.rem(tp, CORES)
     pages = kv.shape[3]
     last = chips - 1
-    up, down, pair = {"tp": tp + CORES}, {"tp": tp - CORES}, {"tp": tp + 1 - 2 * core}
+    corner = jnp.logical_and(z == 0, x == 0)
+    first = jnp.logical_and(corner, core == 0)
+    stand_in = jnp.logical_and(corner, core == 1)
+    usual = jnp.logical_not(corner)
+    above_corner = jnp.logical_and(jnp.logical_and(z == 1, x == 0), core == 0)
+    in_first_row = jnp.logical_and(jnp.logical_and(z == 0, core == 0), x > 0)
+    pair = {"tp": tp + 1 - 2 * core}
+    down = {"tp": tp - CORES + jnp.where(above_corner, 1, 0)}
+    both = jnp.logical_and
+    absent = jnp.logical_not(first)
 
     def seq_rank(steps):
         return lax.rem(x + steps + nx, nx)
 
+    def up(of_core):
+        return {"tp": tp + CORES + of_core - core}
+
     barrier = pltpu.get_barrier_semaphore()
 
-    def greet(device):
-        pl.semaphore_signal(barrier, inc=1, device_id=device, device_id_type=MESH)
-
-    greet(pair)
-    for step in range(1, nx):
-        greet({"seq": seq_rank(step)})
-    pl.when(z < last)(lambda: greet(up))
-    pl.when(z > 0)(lambda: greet(down))
-    pl.semaphore_wait(barrier, nx + jnp.where(z < last, 1, 0) + jnp.where(z > 0, 1, 0))
-
-    def place(plane, kind, of_core):
-        first = ((plane * CORES + of_core) * nx + seq_rank(kind)) * pages
-        return cache.at[:, :, pl.ds(first, pages)]
+    def signal(semaphore, device):
+        pl.semaphore_signal(semaphore, inc=1, device_id=device, device_id_type=MESH)
+
+    @pl.when(absent)
+    def _():
+        signal(barrier, pair)
+        for step in range(1, nx):
+            signal(barrier, {"seq": seq_rank(step)})
+        pl.when(z < last)(lambda: signal(barrier, up(core)))
+        pl.when(in_first_row)(lambda: signal(barrier, {"tp": tp + 1, "seq": 0}))
+        pl.when(above_corner)(lambda: signal(barrier, {"tp": tp - CORES}))
+
+    @pl.when(stand_in)
+    def _():
+        signal(barrier, up(0))
+        for step in range(1, nx):
+            signal(barrier, {"tp": tp - 1, "seq": step})
+
+    greetings = jnp.where(first, nx + 1, jnp.where(stand_in, 2 * (nx - 1), nx + jnp.where(z > 0, 1, 0)))
+    pl.semaphore_wait(barrier, greetings)
+    pl.when(first)(lambda: signal(first_here, pair))
+    pl.when(z > 0)(lambda: signal(up_here, down))
+
+    def index(of_core, plane, kind):
+        return (of_core * chips + plane) * nx + kind
+
+    def place(of_core, plane, kind):
+        start = ((plane * CORES + of_core) * nx + seq_rank(kind)) * pages
+        return cache.at[:, :, pl.ds(start, pages)]
 
     def remote(src, dst, sent, landed, device):
         return pltpu.make_async_remote_copy(
             src_ref=src, dst_ref=dst, send_sem=sent, recv_sem=landed, device_id=device, device_id_type=MESH
         )
 
-    def along(plane, kind, sent, device, src=None):
-        index = plane * nx + kind
-        block = place(plane, kind, core)
-        return remote(block if src is None else src, block, sent.at[index], own_sem.at[index], device)
-
-    def to_pair(plane, kind, src=None):
-        index = plane * nx + kind
-        block = place(plane, kind, core)
-        return remote(block if src is None else src, block, pair_sent.at[index], pair_sem.at[index], pair)
+    def moved(sent, landed, device, of_core, plane, kind, src):
+        at, block = index(of_core, plane, kind), place(of_core, plane, kind)
+        return remote(block if src is None else src, block, sent.at[at], landed.at[at], device)
+
+    def to_up(of_core, plane, kind, src=None):
+        return moved(up_sent, own_sem, up(of_core), of_core, plane, kind, src)
+
+    def to_down(plane, kind, src=None):
+        return moved(down_sent, own_sem, down, core, plane, kind, src)
+
+    def to_pair(of_core, plane, kind, src=None):
+        return moved(pair_sent, pair_sem, pair, of_core, plane, kind, src)
 
     def to_seq(kind):
-        mine = ((z * CORES + core) * nx + x) * pages
         target = seq_rank(-kind)
+        aside = jnp.where(both(in_first_row, target == 0), 1, 0)
+        start = ((z * CORES + core) * nx + x) * pages
         return remote(
             kv.at[:, :, target],
-            cache.at[:, :, pl.ds(mine, pages)],
+            cache.at[:, :, pl.ds(start, pages)],
             x_sent.at[kind],
-            own_sem.at[z * nx + kind],
-            {"seq": target},
+            own_sem.at[index(core, z, kind)],
+            {"tp": tp + aside, "seq": target},
         )
 
     kinds = [0, *sorted(range(1, nx), key=lambda k: (min(k, nx - k), k))]
     mine = kv.at[:, :, x]
-    pl.when(z > 0)(lambda: along(z, 0, down_sent, down, mine).start())
-    pl.when(z < last)(lambda: along(z, 0, up_sent, up, mine).start())
+    pl.when(first)(lambda: to_up(0, 0, 0, mine).start())
+    pl.when(z > 0)(lambda: to_down(z, 0, mine).start())
     for kind in kinds[1:]:
         to_seq(kind).start()
-    local = pltpu.make_async_copy(mine, place(z, 0, core), own_sem.at[z * nx])
+    pl.when(jnp.logical_not(stand_in))(lambda: to_pair(core, z, 0, mine).start())
+    local = pltpu.make_async_copy(mine, place(core, z, 0), local_sem)
     local.start()
-    to_pair(z, 0, mine).start()
-
-    def landed(plane, kind):
-        along(plane, kind, up_sent, up).wait_recv()
+
+    @pl.when(both(absent, z < last))
+    def _():
+        pl.semaphore_wait(up_here, jnp.where(stand_in, 2, 1))
+        to_up(core, z, 0, mine).start()
+
+    def arrive(of_core, plane, kind):
+        to_up(of_core, plane, kind).wait_recv()
+
+    def from_first(of_core, plane, kind):
+        return both(jnp.logical_and(plane == 0, of_core == 0), seq_rank(kind) == 0)
 
     def own(kind):
-        landed(z, kind)
-        pl.when(z > 0)(lambda: along(z, kind, down_sent, down).start())
-        pl.when(z < last)(lambda: along(z, kind, up_sent, up).start())
-        to_pair(z, kind).start()
-
-    def from_above(hops, kind):
-        landed(z + hops, kind)
-        pl.when(z > 0)(lambda: along(z + hops, kind, down_sent, down).start())
-        to_pair(z + hops, kind).start()
-
-    def from_below(hops, kind):
-        landed(z - hops, kind)
-        pl.when(z < last)(lambda: along(z - hops, kind, up_sent, up).start())
-        to_pair(z - hops, kind).start()
-
-    def passing(hops, kind):
-        pl.when(z + hops <= last)(lambda: from_above(hops, kind))
-        pl.when(z - hops >= 0)(lambda: from_below(hops, kind))
+        @pl.when(both(absent, jnp.logical_not(from_first(core, z, kind))))
+        def _():
+            arrive(core, z, kind)
+            pl.when(z > 0)(lambda: to_down(z, kind).start())
+            pl.when(z < last)(lambda: to_up(core, z, kind).start())
+            pl.when(usual)(lambda: to_pair(core, z, kind).start())
+
+        @pl.when(stand_in)
+        def _():
+            arrive(0, z, kind)
+            to_up(0, z, kind).start()
+
+    def passing(hops, kind, first_is_here):
+        @pl.when(both(absent, z + hops <= last))
+        def _():
+            arrive(core, z + hops, kind)
+            pl.when(z > 0)(lambda: to_down(z + hops, kind).start())
+            pl.when(usual)(lambda: to_pair(core, z + hops, kind).start())
+
+            @pl.when(stand_in)
+            def _():
+                arrive(0, hops, kind)
+                if first_is_here:
+                    to_pair(0, hops, kind).start()
+                    to_pair(1, hops, kind).start()
+
+        @pl.when(both(z - hops >= 0, jnp.logical_not(from_first(core, z - hops, kind))))
+        def _():
+            arrive(core, z - hops, kind)
+            pl.when(z < last)(lambda: to_up(core, z - hops, kind).start())
+            to_pair(core, z - hops, kind).start()
+
+    def pass_first():
+        kind = lax.rem(nx - x, nx)
+        arrive(0, 0, kind)
+        pl.when(z < last)(lambda: to_up(0, 0, kind).start())
+        to_pair(0, 0, kind).start()
 
     order = arrival_order(chips, kinds)
+    early = 2 * len(order) // 3
     for kind in kinds[1:-1]:
         own(kind)
-    passing(*order[0])
+    passing(*order[0], False)
     own(kinds[-1])
-    for hops, kind in order[1:]:
-        passing(hops, kind)
+    for hops, kind in order[1:early]:
+        passing(hops, kind, False)
+    pl.when(in_first_row)(pass_first)
+
+    @pl.when(stand_in)
+    def _():
+        pl.semaphore_wait(first_here, 1)
+        to_pair(1, 0, 0, mine).start()
+        for kind in kinds[1:]:
+            to_pair(0, 0, kind).start()
+            to_pair(1, 0, kind).start()
+        for hops, kind in order[:early]:
+            to_pair(0, hops, kind).start()
+            to_pair(1, hops, kind).start()
+
+    for hops, kind in order[early:]:
+        passing(hops, kind, True)
+    pl.when(both(z > 0, core == 0))(pass_first)
 
     local.wait()
     for kind in kinds[1:]:
         to_seq(kind).wait_send()
+    pl.when(first)(lambda: to_up(0, 0, 0).wait_send())
     for plane in range(chips):
         for kind in kinds:
-            to_pair(plane, kind).wait_send()
-            partner_block = place(plane, kind, 1 - core)
-            index = plane * nx + kind
-            remote(partner_block, partner_block, pair_sent.at[index], pair_sem.at[index], pair).wait_recv()
-
-            def sent_down(plane=plane, kind=kind):
-                along(plane, kind, down_sent, down).wait_send()
-
-            def sent_up(plane=plane, kind=kind):
-                along(plane, kind, up_sent, up).wait_send()
-
-            pl.when(jnp.logical_and(z > 0, plane >= z))(sent_down)
-            pl.when(jnp.logical_and(z < last, plane <= z))(sent_up)
+
+            @pl.when(usual)
+            def _(plane=plane, kind=kind):
+                to_pair(core, plane, kind).wait_send()
+                to_pair(1 - core, plane, kind).wait_recv()
+
+            for of_core in range(CORES):
+                if (of_core, plane, kind) != (0, 0, 0):
+                    pl.when(stand_in)(lambda a=(of_core, plane, kind): to_pair(*a).wait_send())
+                    pl.when(first)(lambda a=(of_core, plane, kind): to_pair(*a).wait_recv())
+
+            pl.when(both(z > 0, plane >= z))(lambda a=(plane, kind): to_down(*a).wait_send())
+            pl.when(both(both(absent, z < last), plane <= z))(lambda a=(plane, kind): to_up(core, *a).wait_send())
+    pl.when(first)(lambda: to_pair(0, 0, 0).wait_send())
+
+    @pl.when(stand_in)
+    def _():
+        to_pair(0, 0, 0).wait_recv()
+        for kind in kinds[1:]:
+            to_up(0, 0, kind).wait_send()
 
 
 def attend(length, q, k, v, k_new, v_new):
@@ -208,7 +294,7 @@
     kinds, layers, seqs, positions, head = kv_prefill.shape
     nx = lax.axis_size("seq")
     fan = lax.axis_size("tp") // KVH
-    count = fan // CORES * nx
+    count = fan * nx
     pages = CTX // PAGE
     dma = pltpu.SemaphoreType.DMA
     anywhere = pl.BlockSpec(memory_space=pl.ANY)
@@ -220,7 +306,17 @@
         out_shape=pltpu.VMEM(cache_shape, kv_prefill.dtype),
         in_specs=[pl.BlockSpec(memory_space=pltpu.HBM)],
         out_specs=vmem,
-        scratch_shapes=[dma((count,)), dma((count,)), dma((nx,)), dma((count,)), dma((count,)), dma((count,))],
+        scratch_shapes=[
+            dma((count,)),
+            dma((count,)),
+            dma((nx,)),
+            dma((count,)),
+            dma((count,)),
+            dma((count,)),
+            dma,
+            pltpu.SemaphoreType.REGULAR,
+            pltpu.SemaphoreType.REGULAR,
+        ],
         compiler_params=pltpu.CompilerParams(collective_id=0, has_side_effects=True, vmem_limit_bytes=16 * MIB),
         name="spread",
     )(kv_prefill.reshape(kinds, layers, seqs, positions // PAGE, PAGE, head))

time: 83.2 us -> 62.7 us (0.75)
  the two profiles are of different devices: /device:TPU:33 before, /device:TPU:229 now
where the time goes in v2:
time: 62.7 us; the launch traced here: 62.5 us
  Pallas kernels  60.1 us (96%)
  between operations  1.35 us (2%)
  local copies, waits for them, and re-layouts  1.05 us (2%)
    pallas_call x1, Pallas kernels, body(): pl.pallas_call(spread_kernel, out_shape=pltpu.VMEM(cache_shape, kv_prefil...  55.2 us
    pallas_call x1, Pallas kernels, body(): pl.pallas_call(page_kernel, out_shape=(jax.ShapeDtypeStruct((kinds, layer...  4.93 us

profile of v2, /device:TPU:229, one launch (start us, length us, event | category | flops | bytes accessed | tf_op | source)
XLA Modules:
  0.0 62.5 jit_solution(12238099845334578949)
XLA Ops:
  0.6 0.0 copy-start.2
  0.6 0.0 copy-start.3
  1.3 0.0 copy-start
  1.3 1.0 %copy-done = bf16[2,2,4,128,128]{4,3,2,1,0:T(8,128)(2,1)S(1)} copy-done((bf16[2,2,4,128,128]{4,3,2,1,0:T(8,128)(2,1)S(1)}, bf16[2,2,4,128,128]{4,3,2,1,0:T(8,128)(2,1)}, u32[]{:S(2)}) %copy-start) | copy-done | bytes 524312
  2.4 0.0 copy-start.1
  2.4 55.2 %spread.1.cache = bf16[2,2,256,16,128]{4,3,2,1,0:T(8,128)(2,1)S(1)} custom-call(bf16[2,2,4,8,16,128]{5,4,3,2,1,0:T(8,128)(2,1)S(1)} %bitcast.3), custom_call_target="tpu_custom_call" | custom-call | tf_op jit(solution)/shard_map/spread/pallas_call | solution.py:304
  57.5 0.0 copy-done.2
  57.5 0.0 copy-done.3
  57.6 0.0 copy-done.1
  57.6 4.9 %pages.1 = (bf16[2,2,1,256,16,128]{5,4,3,2,1,0:T(8,128)(2,1)}, bf16[2,128]{1,0:T(2,128)(2,1)}) custom-call(s32[1]{0:T(128)S(6)} %copy.7.lengths, s32[1,256]{1,0:T(1,128)S(1)} %copy-done.2, bf16[2,2,256,16,128]{4,3,2,1,0:T(8,128)(2,1)S(1)} %spread.1.cache, bf16[2,128]{1,0:T(2,128)(2,1)S(1)} %bitcast.4, bf16[2,2,1,8,128]{4,3,2,1,0:T(8,128)(2,1)S(1)} %copy-done.1), custom_call_target="tpu_custom_call" | custom-call | tf_op jit(solution)/shard_map/pages/pallas_call | solution.py:323
Async XLA Ops:
  0.6 56.9 %copy-start.2 = (s32[1,256]{1,0:T(1,128)S(1)}, s32[1,256]{1,0:T(1,128)}, u32[]{:S(2)}) copy-start(s32[1,256]{1,0:T(1,128)} %slots.1) | copy-start | bytes 3076
  0.6 56.9 %copy-start.3 = (bf16[2,1,1,128]{3,0,2,1:T(2,128)(2,1)S(1)}, bf16[2,1,1,128]{3,0,2,1:T(2,128)(2,1)}, u32[]{:S(2)}) copy-start(bf16[2,1,1,128]{3,0,2,1:T(2,128)(2,1)} %param.6) | copy-start | bytes 1540
  1.3 1.0 %copy-start = (bf16[2,2,4,128,128]{4,3,2,1,0:T(8,128)(2,1)S(1)}, bf16[2,2,4,128,128]{4,3,2,1,0:T(8,128)(2,1)}, u32[]{:S(2)}) copy-start(bf16[2,2,4,128,128]{4,3,2,1,0:T(8,128)(2,1)} %param.5) | copy-start | bytes 1572868
  2.4 55.2 %copy-start.1 = (bf16[2,2,1,8,128]{4,3,2,1,0:T(8,128)(2,1)S(1)}, bf16[2,2,1,8,128]{4,3,2,1,0:T(8,128)(2,1)}, u32[]{:S(2)}) copy-start(bf16[2,2,1,8,128]{4,3,2,1,0:T(8,128)(2,1)} %new_kv.1) | copy-start | bytes 24580

commit v3 on v2

--- a/solution.py
+++ b/solution.py
@@ -14,6 +14,7 @@
 CORES = 2
 MESH = pl.DeviceIdType.MESH
 MIB = 1 << 20
+GROUP = 8
 
 
 def arrival_order(chips, kinds):
@@ -26,7 +27,22 @@
 
 
 def spread_kernel(
-    kv, cache, own_sem, pair_sem, x_sent, up_sent, down_sent, pair_sent, local_sem, up_here, first_here
+    kv,
+    cache,
+    own_sem,
+    pair_sem,
+    first_sem,
+    first_pair_sem,
+    x_sent,
+    up_sent,
+    down_sent,
+    pair_sent,
+    first_sent,
+    first_up_sent,
+    first_pair_sent,
+    local_sem,
+    up_here,
+    first_here,
 ):
     tp, x = lax.axis_index("tp"), lax.axis_index("seq")
     ranks, nx = lax.axis_size("tp"), lax.axis_size("seq")
@@ -34,18 +50,18 @@
     chips = fan // CORES
     rank = lax.rem(tp, fan)
     z, core = rank // CORES, lax.rem(tp, CORES)
-    pages = kv.shape[3]
+    layers, pages = kv.shape[1], kv.shape[3]
+    pieces = [(kind, layer) for kind in range(kv.shape[0]) for layer in range(layers)]
     last = chips - 1
-    corner = jnp.logical_and(z == 0, x == 0)
-    first = jnp.logical_and(corner, core == 0)
-    stand_in = jnp.logical_and(corner, core == 1)
-    usual = jnp.logical_not(corner)
-    above_corner = jnp.logical_and(jnp.logical_and(z == 1, x == 0), core == 0)
-    in_first_row = jnp.logical_and(jnp.logical_and(z == 0, core == 0), x > 0)
+    both, no = jnp.logical_and, jnp.logical_not
+    corner = both(z == 0, x == 0)
+    first = both(corner, core == 0)
+    stand_in = both(corner, core == 1)
+    usual, absent = no(corner), no(first)
+    above = both(z == 1, x == 0)
+    row = both(z == 0, x > 0)
     pair = {"tp": tp + 1 - 2 * core}
-    down = {"tp": tp - CORES + jnp.where(above_corner, 1, 0)}
-    both = jnp.logical_and
-    absent = jnp.logical_not(first)
+    down = {"tp": tp - CORES + jnp.where(both(above, core == 0), 1, 0)}
 
     def seq_rank(steps):
         return lax.rem(x + steps + nx, nx)
@@ -53,6 +69,11 @@
     def up(of_core):
         return {"tp": tp + CORES + of_core - core}
 
+    def along_seq(steps):
+        target = seq_rank(steps)
+        aside = jnp.where(both(both(row, core == 0), target == 0), 1, 0)
+        return {"tp": tp + aside, "seq": target}
+
     barrier = pltpu.get_barrier_semaphore()
 
     def signal(semaphore, device):
@@ -62,10 +83,10 @@
     def _():
         signal(barrier, pair)
         for step in range(1, nx):
-            signal(barrier, {"seq": seq_rank(step)})
+            signal(barrier, along_seq(step))
         pl.when(z < last)(lambda: signal(barrier, up(core)))
-        pl.when(in_first_row)(lambda: signal(barrier, {"tp": tp + 1, "seq": 0}))
-        pl.when(above_corner)(lambda: signal(barrier, {"tp": tp - CORES}))
+        pl.when(both(row, core == 1))(lambda: signal(barrier, {"tp": tp - 1, "seq": 0}))
+        pl.when(both(above, core == 1))(lambda: signal(barrier, {"tp": tp - CORES - 1}))
 
     @pl.when(stand_in)
     def _():
@@ -75,15 +96,16 @@
 
     greetings = jnp.where(first, nx + 1, jnp.where(stand_in, 2 * (nx - 1), nx + jnp.where(z > 0, 1, 0)))
     pl.semaphore_wait(barrier, greetings)
-    pl.when(first)(lambda: signal(first_here, pair))
     pl.when(z > 0)(lambda: signal(up_here, down))
 
     def index(of_core, plane, kind):
         return (of_core * chips + plane) * nx + kind
 
+    def start_of(of_core, plane, kind):
+        return ((plane * CORES + of_core) * nx + seq_rank(kind)) * pages
+
     def place(of_core, plane, kind):
-        start = ((plane * CORES + of_core) * nx + seq_rank(kind)) * pages
-        return cache.at[:, :, pl.ds(start, pages)]
+        return cache.at[:, :, pl.ds(start_of(of_core, plane, kind), pages)]
 
     def remote(src, dst, sent, landed, device):
         return pltpu.make_async_remote_copy(
@@ -104,24 +126,67 @@
         return moved(pair_sent, pair_sem, pair, of_core, plane, kind, src)
 
     def to_seq(kind):
-        target = seq_rank(-kind)
-        aside = jnp.where(both(in_first_row, target == 0), 1, 0)
         start = ((z * CORES + core) * nx + x) * pages
         return remote(
-            kv.at[:, :, target],
+            kv.at[:, :, seq_rank(-kind)],
             cache.at[:, :, pl.ds(start, pages)],
             x_sent.at[kind],
             own_sem.at[index(core, z, kind)],
-            {"tp": tp + aside, "seq": target},
+            along_seq(-kind),
         )
 
+    def first_piece(piece):
+        kind, layer = pieces[piece]
+        start = start_of(0, 0, lax.rem(nx - x, nx))
+        return cache.at[kind, layer, pl.ds(start, pages)]
+
+    def first_to(steps, piece, device, sent):
+        kind, layer = pieces[piece]
+        return remote(
+            kv.at[kind, layer, steps],
+            cache.at[kind, layer, pl.ds(0, pages)],
+            first_sent.at[sent * len(pieces) + piece],
+            first_sem.at[piece],
+            device,
+        )
+
+    def first_targets(piece):
+        away = [first_to(k, piece, {"tp": tp + 1, "seq": k}, k) for k in first_order]
+        here = [first_to(0, piece, pair, 0), first_to(0, piece, {"tp": tp + CORES + 1}, nx)]
+        return away, here
+
+    def first_up(piece):
+        block = first_piece(piece)
+        return remote(block, block, first_up_sent.at[piece], first_sem.at[piece], up(core))
+
+    def first_pair(piece):
+        block = first_piece(piece)
+        return remote(block, block, first_pair_sent.at[piece], first_pair_sem.at[piece], pair)
+
     kinds = [0, *sorted(range(1, nx), key=lambda k: (min(k, nx - k), k))]
+    first_order = kinds[1:]
     mine = kv.at[:, :, x]
-    pl.when(first)(lambda: to_up(0, 0, 0, mine).start())
+
+    @pl.when(first)
+    def _():
+        signal(first_here, pair)
+        sends = [first_targets(piece) for piece in range(len(pieces))]
+        for _, here in sends:
+            here[1].start()
+        for place_in_order in range(nx - 1):
+            for away, _ in sends:
+                away[place_in_order].start()
+        for _, here in sends:
+            here[0].start()
+
     pl.when(z > 0)(lambda: to_down(z, 0, mine).start())
-    for kind in kinds[1:]:
-        to_seq(kind).start()
-    pl.when(jnp.logical_not(stand_in))(lambda: to_pair(core, z, 0, mine).start())
+
+    @pl.when(absent)
+    def _():
+        for kind in kinds[1:]:
+            to_seq(kind).start()
+
+    pl.when(usual)(lambda: to_pair(core, z, 0, mine).start())
     local = pltpu.make_async_copy(mine, place(core, z, 0), local_sem)
     local.start()
 
@@ -134,10 +199,10 @@
         to_up(of_core, plane, kind).wait_recv()
 
     def from_first(of_core, plane, kind):
-        return both(jnp.logical_and(plane == 0, of_core == 0), seq_rank(kind) == 0)
+        return both(both(plane == 0, of_core == 0), seq_rank(kind) == 0)
 
     def own(kind):
-        @pl.when(both(absent, jnp.logical_not(from_first(core, z, kind))))
+        @pl.when(both(absent, no(from_first(core, z, kind))))
         def _():
             arrive(core, z, kind)
             pl.when(z > 0)(lambda: to_down(z, kind).start())
@@ -163,17 +228,17 @@
                     to_pair(0, hops, kind).start()
                     to_pair(1, hops, kind).start()
 
-        @pl.when(both(z - hops >= 0, jnp.logical_not(from_first(core, z - hops, kind))))
+        @pl.when(both(z - hops >= 0, no(from_first(core, z - hops, kind))))
         def _():
             arrive(core, z - hops, kind)
             pl.when(z < last)(lambda: to_up(core, z - hops, kind).start())
             to_pair(core, z - hops, kind).start()
 
     def pass_first():
-        kind = lax.rem(nx - x, nx)
-        arrive(0, 0, kind)
-        pl.when(z < last)(lambda: to_up(0, 0, kind).start())
-        to_pair(0, 0, kind).start()
+        for piece in range(len(pieces)):
+            first_up(piece).wait_recv()
+            pl.when(both(z < last, usual))(lambda: first_up(piece).start())
+            pl.when(usual)(lambda: first_pair(piece).start())
 
     order = arrival_order(chips, kinds)
     early = 2 * len(order) // 3
@@ -183,7 +248,7 @@
     own(kinds[-1])
     for hops, kind in order[1:early]:
         passing(hops, kind, False)
-    pl.when(in_first_row)(pass_first)
+    pl.when(both(row, core == 1))(pass_first)
 
     @pl.when(stand_in)
     def _():
@@ -198,18 +263,24 @@
 
     for hops, kind in order[early:]:
         passing(hops, kind, True)
-    pl.when(both(z > 0, core == 0))(pass_first)
+    pl.when(both(jnp.logical_or(z > 0, stand_in), core == 1))(pass_first)
 
     local.wait()
-    for kind in kinds[1:]:
-        to_seq(kind).wait_send()
-    pl.when(first)(lambda: to_up(0, 0, 0).wait_send())
+
+    @pl.when(absent)
+    def _():
+        for kind in kinds[1:]:
+            to_seq(kind).wait_send()
+
     for plane in range(chips):
         for kind in kinds:
 
-            @pl.when(usual)
+            @pl.when(both(usual, no(from_first(core, plane, kind))))
             def _(plane=plane, kind=kind):
                 to_pair(core, plane, kind).wait_send()
+
+            @pl.when(both(usual, no(from_first(1 - core, plane, kind))))
+            def _(plane=plane, kind=kind):
                 to_pair(1 - core, plane, kind).wait_recv()
 
             for of_core in range(CORES):
@@ -218,12 +289,28 @@
                     pl.when(first)(lambda a=(of_core, plane, kind): to_pair(*a).wait_recv())
 
             pl.when(both(z > 0, plane >= z))(lambda a=(plane, kind): to_down(*a).wait_send())
-            pl.when(both(both(absent, z < last), plane <= z))(lambda a=(plane, kind): to_up(core, *a).wait_send())
-    pl.when(first)(lambda: to_pair(0, 0, 0).wait_send())
+
+            @pl.when(both(both(absent, z < last), both(plane <= z, no(from_first(core, plane, kind)))))
+            def _(plane=plane, kind=kind):
+                to_up(core, plane, kind).wait_send()
+
+    for piece in range(len(pieces)):
+
+        @pl.when(both(usual, core == 1))
+        def _(piece=piece):
+            pl.when(z < last)(lambda: first_up(piece).wait_send())
+            first_pair(piece).wait_send()
+
+        pl.when(both(usual, core == 0))(lambda: first_pair(piece).wait_recv())
+
+        @pl.when(first)
+        def _(piece=piece):
+            away, here = first_targets(piece)
+            for copy in away + here:
+                copy.wait_send()
 
     @pl.when(stand_in)
     def _():
-        to_pair(0, 0, 0).wait_recv()
         for kind in kinds[1:]:
             to_up(0, 0, kind).wait_send()
 
@@ -247,35 +334,42 @@
     return mixed[:1].astype(jnp.bfloat16)
 
 
-def page_kernel(lengths, slots, cache, queries, new_kv, pool, out, staged, sem):
-    layers, pages, head = cache.shape[1], cache.shape[2], cache.shape[4]
+def page_kernel(lengths, slots, cache, queries, new_kv, pool, out, tile, sem, tile_sem):
+    kinds, layers, pages, head = cache.shape[0], cache.shape[1], cache.shape[2], cache.shape[4]
     length = lengths[0]
-    slot_now, row_now = slots[0, length // PAGE], lax.rem(length, PAGE)
+    page_now, row_now = length // PAGE, lax.rem(length, PAGE)
     head_now = lax.axis_index("tp") * KVH // lax.axis_size("tp")
     rows = lax.broadcasted_iota(jnp.int32, (PAGE, head), 0)
 
     def fresh(kind, layer):
         block = new_kv[kind, layer, 0].astype(jnp.float32)
         mine = lax.broadcasted_iota(jnp.int32, block.shape, 0) == head_now
-        return jnp.sum(jnp.where(mine, block, 0.0), axis=0, keepdims=True).astype(jnp.bfloat16)
-
-    copies = []
-    for kind in range(2):
+        return jnp.sum(jnp.where(mine, block, 0.0), axis=0, keepdims=True)
+
+    for kind in range(kinds):
         for layer in range(layers):
-
-            def move(page, _, kind=kind, layer=layer):
-                staged[kind, layer, slots[0, page]] = cache[kind, layer, page]
-                return 0
-
-            lax.fori_loop(0, pages, move, 0, unroll=16)
-            tile = staged[kind, layer, slot_now].astype(jnp.float32)
-            tile = jnp.where(rows == row_now, fresh(kind, layer).astype(jnp.float32), tile)
-            staged[kind, layer, slot_now] = tile.astype(jnp.bfloat16)
-            copy = pltpu.make_async_copy(
-                staged.at[kind, layer], pool.at[kind, layer, 0], sem.at[kind * layers + layer]
-            )
-            copy.start()
-            copies.append(copy)
+            held = cache[kind, layer, page_now].astype(jnp.float32)
+            tile[kind, layer] = jnp.where(rows == row_now, fresh(kind, layer), held).astype(tile.dtype)
+
+    def place(page):
+        return pool.at[:, :, 0, slots[0, page]]
+
+    def put(page):
+        pltpu.make_async_copy(cache.at[:, :, page], place(page), sem).start()
+
+    def put_group(group, _):
+        @pl.when(group != page_now // GROUP)
+        def _():
+            for page in range(GROUP):
+                put(group * GROUP + page)
+
+        return 0
+
+    lax.fori_loop(0, pages // GROUP, put_group, 0)
+    for step in range(1, GROUP):
+        put(page_now // GROUP * GROUP + lax.rem(page_now + step, GROUP))
+    placed = pltpu.make_async_copy(tile, place(page_now), tile_sem)
+    placed.start()
 
     for layer in range(layers):
         out[layer : layer + 1] = attend(
@@ -283,11 +377,12 @@
             queries[layer : layer + 1],
             cache[0, layer].reshape(CTX, head),
             cache[1, layer].reshape(CTX, head),
-            fresh(0, layer),
-            fresh(1, layer),
+            fresh(0, layer).astype(queries.dtype),
+            fresh(1, layer).astype(queries.dtype),
         )
-    for copy in copies:
-        copy.wait()
+    others = cache.at[:, :, pl.ds(1, pages - 1)]
+    pltpu.make_async_copy(others, pool.at[:, :, 0, pl.ds(1, pages - 1)], sem).wait()
+    placed.wait()
 
 
 def body(kv_prefill, queries, new_kv, lengths, page_slots):
@@ -296,11 +391,13 @@
     fan = lax.axis_size("tp") // KVH
     count = fan * nx
     pages = CTX // PAGE
+    pieces = kinds * layers
     dma = pltpu.SemaphoreType.DMA
     anywhere = pl.BlockSpec(memory_space=pl.ANY)
     vmem = pl.BlockSpec(memory_space=pltpu.VMEM)
     smem = pl.BlockSpec(memory_space=pltpu.SMEM)
     cache_shape = (kinds, layers, pages, PAGE, head)
+    blocks = kv_prefill.reshape(kinds, layers, seqs, positions // PAGE, PAGE, head)
     cache = pl.pallas_call(
         spread_kernel,
         out_shape=pltpu.VMEM(cache_shape, kv_prefill.dtype),
@@ -309,17 +406,22 @@
         scratch_shapes=[
             dma((count,)),
             dma((count,)),
+            dma((pieces,)),
+            dma((pieces,)),
             dma((nx,)),
             dma((count,)),
             dma((count,)),
             dma((count,)),
+            dma(((nx + 1) * pieces,)),
+            dma((pieces,)),
+            dma((pieces,)),
             dma,
             pltpu.SemaphoreType.REGULAR,
             pltpu.SemaphoreType.REGULAR,
         ],
         compiler_params=pltpu.CompilerParams(collective_id=0, has_side_effects=True, vmem_limit_bytes=16 * MIB),
         name="spread",
-    )(kv_prefill.reshape(kinds, layers, seqs, positions // PAGE, PAGE, head))
+    )(pltpu.with_memory_space_constraint(blocks, pltpu.HBM))
     pool, out = pl.pallas_call(
         page_kernel,
         out_shape=(
@@ -328,7 +430,7 @@
         ),
         in_specs=[smem, smem, vmem, vmem, vmem],
         out_specs=(anywhere, vmem),
-        scratch_shapes=[pltpu.VMEM(cache_shape, kv_prefill.dtype), dma((kinds * layers,))],
+        scratch_shapes=[pltpu.VMEM((kinds, layers, PAGE, head), kv_prefill.dtype), dma, dma],
         compiler_params=pltpu.CompilerParams(vmem_limit_bytes=24 * MIB),
         name="pages",
     )(lengths, page_slots, cache, queries.reshape(layers, head), new_kv)

time: 62.7 us -> 56.5 us (0.901)
  the two profiles are of different devices: /device:TPU:229 before, /device:TPU:33 now
where the time goes in v3:
time: 56.5 us; the launch traced here: 56.3 us
  Pallas kernels  55 us (97%)
  between operations  1.36 us (2%)
    pallas_call x1, Pallas kernels, body(): pl.pallas_call(spread_kernel, out_shape=pltpu.VMEM(cache_shape, kv_prefil...  50.8 us
    pallas_call x1, Pallas kernels, body(): pl.pallas_call(page_kernel, out_shape=(jax.ShapeDtypeStruct((kinds, layer...  4.14 us

profile of v3, /device:TPU:33, one launch (start us, length us, event | category | flops | bytes accessed | tf_op | source)
XLA Modules:
  0.0 56.3 jit_solution(14550750319467940046)
XLA Ops:
  0.6 0.0 copy-start.1
  0.6 0.0 copy-start
  0.7 0.0 copy-start.2
  1.3 50.8 %spread.1.cache = bf16[2,2,256,16,128]{4,3,2,1,0:T(8,128)(2,1)S(1)} custom-call(bf16[2,2,4,8,16,128]{5,4,3,2,1,0:T(8,128)(2,1)} %bitcast.4), custom_call_target="tpu_custom_call" | custom-call | tf_op jit(solution)/shard_map/spread/pallas_call | solution.py:401
  52.2 0.0 copy-done.1
  52.2 0.0 copy-done
  52.2 0.0 copy-done.2
  52.2 4.1 %pages.1 = (bf16[2,2,1,256,16,128]{5,4,3,2,1,0:T(8,128)(2,1)}, bf16[2,128]{1,0:T(2,128)(2,1)}) custom-call(s32[1]{0:T(128)S(6)} %copy.7.lengths, s32[1,256]{1,0:T(1,128)S(1)} %copy-done.1, bf16[2,2,256,16,128]{4,3,2,1,0:T(8,128)(2,1)S(1)} %spread.1.cache, bf16[2,128]{1,0:T(2,128)(2,1)S(1)} %bitcast.3, bf16[2,2,1,8,128]{4,3,2,1,0:T(8,128)(2,1)S(1)} %copy-done), custom_call_target="tpu_custom_call" | custom-call | tf_op jit(solution)/shard_map/pages/pallas_call | solution.py:425
Async XLA Ops:
  0.6 51.5 %copy-start.1 = (s32[1,256]{1,0:T(1,128)S(1)}, s32[1,256]{1,0:T(1,128)}, u32[]{:S(2)}) copy-start(s32[1,256]{1,0:T(1,128)} %slots.1) | copy-start | bytes 3076
  0.6 51.5 %copy-start = (bf16[2,2,1,8,128]{4,3,2,1,0:T(8,128)(2,1)S(1)}, bf16[2,2,1,8,128]{4,3,2,1,0:T(8,128)(2,1)}, u32[]{:S(2)}) copy-start(bf16[2,2,1,8,128]{4,3,2,1,0:T(8,128)(2,1)} %new_kv.1) | copy-start | bytes 24580
  0.7 51.5 %copy-start.2 = (bf16[2,1,1,128]{3,0,2,1:T(2,128)(2,1)S(1)}, bf16[2,1,1,128]{3,0,2,1:T(2,128)(2,1)}, u32[]{:S(2)}) copy-start(bf16[2,1,1,128]{3,0,2,1:T(2,128)(2,1)} %param.6) | copy-start | bytes 1540

commit v4 on v3

v4 whole, which is shorter than its diff:
```python
import functools
import math

import jax
import jax.numpy as jnp
from jax import lax
from jax.experimental import pallas as pl
from jax.experimental.pallas import tpu as pltpu
from jax.sharding import PartitionSpec as P

KVH = 8
PAGE = 16
CTX = 4096
CORES = 2
MESH = pl.DeviceIdType.MESH
MIB = 1 << 20


def arrival_order(chips, kinds):
    order = []
    for _ in range(chips - 1):
        further = [(hops + 1, kind) for hops, kind in order]
        own = [(1, kind) for kind in kinds]
        order = own[:-1] + further[:1] + own[-1:] + further[1:]
    return order


def spread_kernel(
    kv,
    slots,
    queries,
    new_kv,
    cache,
    slots_here,
    queries_here,
    new_kv_here,
    own_sem,
    pair_sem,
    first_sem,
    first_pair_sem,
    bulk_sem,
    x_sent,
    up_sent,
    down_sent,
    pair_sent,
    first_sent,
    first_up_sent,
    first_pair_sent,
    bulk_sent,
    local_sem,
    small_sem,
    up_here,
    first_here,
):
    tp, x = lax.axis_index("tp"), lax.axis_index("seq")
    ranks, nx = lax.axis_size("tp"), lax.axis_size("seq")
    fan = ranks // KVH
    chips = fan // CORES
    rank = lax.rem(tp, fan)
    z, core = rank // CORES, lax.rem(tp, CORES)
    layers, pages = kv.shape[1], kv.shape[3]
    pieces = [(kind, layer) for kind in range(kv.shape[0]) for layer in range(layers)]
    last = chips - 1
    both, no = jnp.logical_and, jnp.logical_not
    corner = both(z == 0, x == 0)
    first = both(corner, core == 0)
    stand_in = both(corner, core == 1)
    usual, absent = no(corner), no(first)
    above = both(z == 1, x == 0)
    row = both(z == 0, x > 0)
    pair = {"tp": tp + 1 - 2 * core}
    down = {"tp": tp - CORES + jnp.where(both(above, core == 0), 1, 0)}

    def seq_rank(steps):
        return lax.rem(x + steps + nx, nx)

    def up(of_core):
        return {"tp": tp + CORES + of_core - core}

    def along_seq(steps):
        target = seq_rank(steps)
        aside = jnp.where(both(both(row, core == 0), target == 0), 1, 0)
        return {"tp": tp + aside, "seq": target}

    barrier = pltpu.get_barrier_semaphore()

    def signal(semaphore, device):
        pl.semaphore_signal(semaphore, inc=1, device_id=device, device_id_type=MESH)

    @pl.when(absent)
    def _():
        signal(barrier, pair)
        for step in range(1, nx):
            signal(barrier, along_seq(step))
        pl.when(z < last)(lambda: signal(barrier, up(core)))
        pl.when(both(row, core == 1))(lambda: signal(barrier, {"tp": tp - 1, "seq": 0}))
        pl.when(both(above, core == 1))(lambda: signal(barrier, {"tp": tp - CORES - 1}))

    @pl.when(stand_in)
    def _():
        signal(barrier, up(0))
        for step in range(1, nx):
            signal(barrier, {"tp": tp - 1, "seq": step})

    greetings = jnp.where(first, nx + 1, jnp.where(stand_in, 2 * (nx - 1), nx + jnp.where(z > 0, 1, 0)))
    pl.semaphore_wait(barrier, greetings)
    pl.when(z > 0)(lambda: signal(up_here, down))

    def index(of_core, plane, kind):
        return (of_core * chips + plane) * nx + kind

    def start_of(of_core, plane, kind):
        return ((plane * CORES + of_core) * nx + seq_rank(kind)) * pages

    def place(of_core, plane, kind):
        return cache.at[:, :, pl.ds(start_of(of_core, plane, kind), pages)]

    def remote(src, dst, sent, landed, device):
        return pltpu.make_async_remote_copy(
            src_ref=src, dst_ref=dst, send_sem=sent, recv_sem=landed, device_id=device, device_id_type=MESH
        )

    def moved(sent, landed, device, of_core, plane, kind, src):
        block = place(of_core, plane, kind)
        return remote(block if src is None else src, block, sent, landed, device)

    def to_up(of_core, plane, kind, src=None):
        at = own_sem.at[index(of_core, plane, kind)]
        return moved(up_sent.at[plane], at, up(of_core), of_core, plane, kind, src)

    def to_down(plane, kind, src=None):
        at = own_sem.at[index(core, plane, kind)]
        return moved(down_sent.at[plane], at, down, core, plane, kind, src)

    def to_pair(plane, kind, src=None):
        return moved(pair_sent.at[plane], pair_sem.at[plane], pair, core, plane, kind, src)

    def to_first_one(of_core, plane, kind):
        return moved(bulk_sent, bulk_sem, pair, of_core, plane, kind, None)

    def blocks(count, semaphore):
        every = cache.at[:, :, pl.ds(0, count * pages)]
        return remote(every, every, semaphore, semaphore, pair)

    def to_seq(kind):
        start = ((z * CORES + core) * nx + x) * pages
        return remote(
            kv.at[:, :, seq_rank(-kind)],
            cache.at[:, :, pl.ds(start, pages)],
            x_sent,
            own_sem.at[index(core, z, kind)],
            along_seq(-kind),
        )

    def first_piece(piece):
        kind, layer = pieces[piece]
        start = start_of(0, 0, lax.rem(nx - x, nx))
        return cache.at[kind, layer, pl.ds(start, pages)]

    def first_to(steps, piece, device):
        kind, layer = pieces[piece]
        return remote(
            kv.at[kind, layer, steps],
            cache.at[kind, layer, pl.ds(0, pages)],
            first_sent,
            first_sem.at[piece],
            device,
        )

    def first_up(piece):
        block = first_piece(piece)
        return remote(block, block, first_up_sent, first_sem.at[piece], up(core))

    def first_pair(piece):
        block = first_piece(piece)
        return remote(block, block, first_pair_sent, first_pair_sem, pair)

    kinds = [0, *sorted(range(1, nx), key=lambda k: (min(k, nx - k), k))]
    mine = kv.at[:, :, x]

    @pl.when(first)
    def _():
        signal(first_here, pair)
        away = [(k, {"tp": tp + 1, "seq": k}) for k in kinds[1:]]
        for steps, device in [away[-1], (0, {"tp": tp + CORES + 1}), *away[:-1], (0, pair)]:
            for piece in range(len(pieces)):
                first_to(steps, piece, device).start()

    pl.when(z > 0)(lambda: to_down(z, 0, mine).start())

    @pl.when(absent)
    def _():
        for kind in kinds[1:]:
            to_seq(kind).start()

    pl.when(usual)(lambda: to_pair(z, 0, mine).start())
    local = pltpu.make_async_copy(mine, place(core, z, 0), local_sem)
    local.start()
    small = [(slots, slots_here), (queries, queries_here), (new_kv, new_kv_here)]
    small = [pltpu.make_async_copy(*ends, small_sem.at[at]) for at, ends in enumerate(small)]
    for copy in small:
        copy.start()

    @pl.when(both(absent, z < last))
    def _():
        pl.semaphore_wait(up_here, jnp.where(stand_in, 2, 1))
        to_up(core, z, 0, mine).start()

    def arrive(of_core, plane, kind):
        to_up(of_core, plane, kind).wait_recv()

    def from_first(of_core, plane, kind):
        return both(both(plane == 0, of_core == 0), seq_rank(kind) == 0)

    def own(kind):
        @pl.when(both(absent, no(from_first(core, z, kind))))
        def _():
            arrive(core, z, kind)
            pl.when(z > 0)(lambda: to_down(z, kind).start())
            pl.when(z < last)(lambda: to_up(core, z, kind).start())
            pl.when(usual)(lambda: to_pair(z, kind).start())

        @pl.when(stand_in)
        def _():
            arrive(0, z, kind)
            to_up(0, z, kind).start()

    def passing(hops, kind, first_is_here):
        @pl.when(both(absent, z + hops <= last))
        def _():
            arrive(core, z + hops, kind)
            pl.when(z > 0)(lambda: to_down(z + hops, kind).start())
            pl.when(usual)(lambda: to_pair(z + hops, kind).start())

            @pl.when(stand_in)
            def _():
                arrive(0, hops, kind)
                if first_is_here:
                    to_first_one(0, hops, kind).start()
                    to_first_one(1, hops, kind).start()

        @pl.when(both(z - hops >= 0, no(from_first(core, z - hops, kind))))
        def _():
            arrive(core, z - hops, kind)
            pl.when(z < last)(lambda: to_up(core, z - hops, kind).start())
            to_pair(z - hops, kind).start()

    def pass_first():
        for piece in range(len(pieces)):
            first_up(piece).wait_recv()
            pl.when(both(z < last, usual))(lambda: first_up(piece).start())
            pl.when(usual)(lambda: first_pair(piece).start())

    def to_first(piece):
        kind, layer = pieces[piece]
        block = cache.at[kind, layer, pl.ds(pages, (last * CORES * nx - 1) * pages)]
        return remote(block, block, bulk_sent, bulk_sem, pair)

    order = arrival_order(chips, kinds)
    for kind in kinds[1:-1]:
        own(kind)
    near = max(at for at, (hops, _) in enumerate(order) if hops < last)
    for at, (hops, kind) in enumerate(order):
        passing(hops, kind, at > near)
        if at == 0:
            own(kinds[-1])
        if at == near:

            @pl.when(stand_in)
            def _():
                local.wait()
                pl.semaphore_wait(first_here, 1)
                for piece in range(len(pieces)):
                    to_first(piece).start()
                for far, of_kind in order[:at]:
                    if far == last:
                        to_first_one(0, far, of_kind).start()
                        to_first_one(1, far, of_kind).start()

        if at == len(order) - 3:
            pl.when(both(row, core == 1))(pass_first)
    for copy in small:
        copy.wait()
    pl.when(no(stand_in))(lambda: local.wait())
    pl.when(absent)(lambda: blocks(nx - 1, x_sent).wait_send())

    @pl.when(usual)
    def _():
        for plane in range(1, chips):
            blocks(nx, pair_sem.at[plane]).wait_recv()
            blocks(nx, pair_sent.at[plane]).wait_send()

        @pl.when(core == 0)
        def _():
            blocks(nx, pair_sem.at[0]).wait_recv()
            blocks(nx - 1, pair_sent.at[0]).wait_send()

        @pl.when(core == 1)
        def _():
            blocks(nx - 1, pair_sem.at[0]).wait_recv()
            blocks(nx, pair_sent.at[0]).wait_send()

    pl.when(both(jnp.logical_or(z > 0, stand_in), core == 1))(pass_first)

    for plane in range(chips):
        pl.when(both(z > 0, plane >= z))(lambda: blocks(nx, down_sent.at[plane]).wait_send())
    for plane in range(1, last):
        pl.when(both(z < last, plane <= z))(lambda: blocks(nx, up_sent.at[plane]).wait_send())
    below = both(usual, z < last)
    pl.when(both(below, core == 0))(lambda: blocks(nx - 1, up_sent.at[0]).wait_send())
    pl.when(both(below, core == 1))(lambda: blocks(nx, up_sent.at[0]).wait_send())
    pl.when(both(below, core == 1))(lambda: blocks(1, first_up_sent).wait_send())
    pl.when(both(usual, core == 1))(lambda: blocks(1, first_pair_sent).wait_send())
    pl.when(both(usual, core == 0))(lambda: blocks(1, first_pair_sem).wait_recv())
    handed = chips * CORES * nx - 1

    @pl.when(stand_in)
    def _():
        blocks(2 * nx - 1, up_sent.at[0]).wait_send()
        blocks(handed, bulk_sent).wait_send()

    @pl.when(first)
    def _():
        blocks(nx + 1, first_sent).wait_send()
        blocks(handed, bulk_sem).wait_recv()


def attend(length, queries, cache, fresh):
    layers, head = queries.shape
    scale = 1.0 / math.sqrt(head)
    every = range(layers)
    keys = [cache[0, layer].reshape(CTX, head) for layer in every]
    values = [cache[1, layer].reshape(CTX, head) for layer in every]
    q = [jnp.broadcast_to(queries[layer : layer + 1], (8, head)) for layer in every]
    contract = (((1,), (1,)), ((), ()))
    scores = [lax.dot_general(q[i], keys[i], contract, preferred_element_type=jnp.float32) * scale for i in every]
    new = [jnp.sum(q[i].astype(jnp.float32) * fresh(0, i), axis=1, keepdims=True) * scale for i in every]
    visible = lax.broadcasted_iota(jnp.int32, scores[0].shape, 1) < length
    scores = [jnp.where(visible, s, -1e30) for s in scores]
    top = [jnp.maximum(jnp.max(s, axis=1, keepdims=True), n) for s, n in zip(scores, new)]
    weights = [jnp.where(visible, jnp.exp(s - t), 0.0) for s, t in zip(scores, top)]
    new = [jnp.exp(n - t) for n, t in zip(new, top)]
    total = [jnp.sum(w, axis=1, keepdims=True) + n for w, n in zip(weights, new)]
    mixed = [jnp.dot(weights[i].astype(values[i].dtype), values[i], preferred_element_type=jnp.float32) for i in every]
    return [(mixed[i] + new[i] * fresh(1, i)) / total[i] for i in every]


def page_kernel(lengths, slots, cache, queries, new_kv, pool, out, tile, sem, tile_sem):
    kinds, layers, pages, head = cache.shape[0], cache.shape[1], cache.shape[2], cache.shape[4]
    length = lengths[0]
    page_now, row_now = length // PAGE, lax.rem(length, PAGE)
    head_now = lax.axis_index("tp") * KVH // lax.axis_size("tp")
    rows = lax.broadcasted_iota(jnp.int32, (PAGE, head), 0)

    def place(page):
        return pool.at[:, :, 0, slots[0, page]]

    def put(step, _):
        page = lax.rem(page_now + step, pages)
        pltpu.make_async_copy(cache.at[:, :, page], place(page), sem).start()
        return 0

    lax.fori_loop(1, pages, put, 0, unroll=15)

    def fresh(kind, layer):
        block = new_kv[kind, layer, 0].astype(jnp.float32)
        mine = lax.broadcasted_iota(jnp.int32, block.shape, 0) == head_now
        return jnp.sum(jnp.where(mine, block, 0.0), axis=0, keepdims=True)

    for kind in range(kinds):
        for layer in range(layers):
            held = cache[kind, layer, page_now].astype(jnp.float32)
            tile[kind, layer] = jnp.where(rows == row_now, fresh(kind, layer), held).astype(tile.dtype)
    placed = pltpu.make_async_copy(tile, place(page_now), tile_sem)
    placed.start()
    for layer, mixed in enumerate(attend(length, queries, cache, fresh)):
        out[layer : layer + 1] = mixed[:1].astype(out.dtype)
    others = pl.ds(1, pages - 1)
    pltpu.make_async_copy(cache.at[:, :, others], pool.at[:, :, 0, others], sem).wait()
    placed.wait()


def body(kv_prefill, queries, new_kv, lengths, page_slots):
    kinds, layers, seqs, positions, head = kv_prefill.shape
    nx = lax.axis_size("seq")
    fan = lax.axis_size("tp") // KVH
    chips = fan // CORES
    pages = CTX // PAGE
    pieces = kinds * layers
    dma = pltpu.SemaphoreType.DMA
    anywhere = pl.BlockSpec(memory_space=pl.ANY)
    vmem = pl.BlockSpec(memory_space=pltpu.VMEM)
    smem = pl.BlockSpec(memory_space=pltpu.SMEM)
    cache_shape = (kinds, layers, pages, PAGE, head)
    blocks = kv_prefill.reshape(kinds, layers, seqs, positions // PAGE, PAGE, head)
    hbm = pl.BlockSpec(memory_space=pltpu.HBM)
    small = (page_slots, queries.reshape(layers, head), new_kv)
    cache, *small = pl.pallas_call(
        spread_kernel,
        out_shape=(
            pltpu.VMEM(cache_shape, kv_prefill.dtype),
            pltpu.SMEM(page_slots.shape, page_slots.dtype),
            pltpu.VMEM((layers, head), queries.dtype),
            pltpu.VMEM(new_kv.shape, new_kv.dtype),
        ),
        in_specs=[hbm] * 4,
        out_specs=(vmem, smem, vmem, vmem),
        scratch_shapes=[
            dma((fan * nx,)),
            dma((chips,)),
            dma((pieces,)),
            dma,
            dma,
            dma,
            dma((chips,)),
            dma((chips,)),
            dma((chips,)),
            dma,
            dma,
            dma,
            dma,
            dma,
            dma((3,)),
            pltpu.SemaphoreType.REGULAR,
            pltpu.SemaphoreType.REGULAR,
        ],
        compiler_params=pltpu.CompilerParams(collective_id=0, has_side_effects=True, vmem_limit_bytes=16 * MIB),
        name="spread",
    )(*(pltpu.with_memory_space_constraint(a, pltpu.HBM) for a in (blocks, *small)))
    pool, out = pl.pallas_call(
        page_kernel,
        out_shape=(
            jax.ShapeDtypeStruct((kinds, layers, 1, pages, PAGE, head), kv_prefill.dtype),
            jax.ShapeDtypeStruct((layers, head), queries.dtype),
        ),
        in_specs=[smem, smem, vmem, vmem, vmem],
        out_specs=(anywhere, vmem),
        scratch_shapes=[pltpu.VMEM((kinds, layers, PAGE, head), kv_prefill.dtype), dma, dma],
        compiler_params=pltpu.CompilerParams(vmem_limit_bytes=24 * MIB),
        name="pages",
    )(lengths, small[0], cache, *small[1:])
    return pool, out.reshape(queries.shape)


def solution(mesh):
    placed = (
        P(None, None, "groups", ("tp", "seq"), None),
        P(None, ("groups", "seq"), "tp", None),
        P(None, None, ("groups", "seq"), None, None),
        P(("groups", "seq")),
        P(("groups", "seq"), None),
    )
    return jax.shard_map(
        body,
        mesh=mesh,
        in_specs=placed,
        out_specs=(
            P(None, None, "tp", ("groups", "seq"), None, None),
            P(None, ("groups", "seq"), "tp", None),
        ),
        check_vma=False,
    )
```

time: 56.5 us -> 54 us (0.956)
  Pallas kernels: 55 us -> 52.6 us
    pallas_call x1, Pallas kernels: 50.8 us -> 49.4 us  [body(): pl.pallas_call(spread_kernel, out_shape=(pltpu.VMEM(cache_shape, kv_prefi...]
    pallas_call x1, Pallas kernels: 4.14 us -> 3.21 us  [body(): pl.pallas_call(page_kernel, out_shape=(jax.ShapeDtypeStruct((kinds, layer...]
where the time goes in v4:
time: 54 us; the launch traced here: 53.9 us
  Pallas kernels  52.6 us (97%)
  between operations  1.29 us (2%)
    pallas_call x1, Pallas kernels, body(): pl.pallas_call(spread_kernel, out_shape=(pltpu.VMEM(cache_shape, kv_prefi...  49.4 us
    pallas_call x1, Pallas kernels, body(): pl.pallas_call(page_kernel, out_shape=(jax.ShapeDtypeStruct((kinds, layer...  3.21 us

profile of v4, /device:TPU:33, one launch (start us, length us, event | category | flops | bytes accessed | tf_op | source)
XLA Modules:
  0.0 53.9 jit_solution(4796217653135185659)
XLA Ops:
  1.3 49.4 %spread.1 = (bf16[2,2,256,16,128]{4,3,2,1,0:T(8,128)(2,1)S(1)}, s32[1,256]{1,0:T(1,128)S(4)}, bf16[2,128]{1,0:T(2,128)(2,1)S(1)}, bf16[2,2,1,8,128]{4,3,2,1,0:T(8,128)(2,1)S(1)}) custom-call(bf16[2,2,4,8,16,128]{5,4,3,2,1,0:T(8,128)(2,1)} %bitcast.3, s32[1,256]{1,0:T(1,128)} %slots.1, bf16[2,128]{1,0:T(2,128)(2,1)} %bitcast.4, bf16[2,2,1,8,128]{4,3,2,1,0:T(8,128)(2,1)} %new_kv.1), custom_call_target="tpu_custom_call" | custom-call | tf_op jit(solution)/shard_map/spread/pallas_call | solution.py:398
  50.7 3.2 %pages.1 = (bf16[2,2,1,256,16,128]{5,4,3,2,1,0:T(8,128)(2,1)}, bf16[2,128]{1,0:T(2,128)(2,1)}) custom-call(s32[1]{0:T(128)S(6)} %copy.7.lengths, s32[1,256]{1,0:T(1,128)S(4)} %get-tuple-element.8.slots, bf16[2,2,256,16,128]{4,3,2,1,0:T(8,128)(2,1)S(1)} %get-tuple-element.9.cache, bf16[2,128]{1,0:T(2,128)(2,1)S(1)} %get-tuple-element.10.queries, ...), custom_call_target="tpu_custom_call" | custom-call | tf_op jit(solution)/shard_map/pages/pallas_call | solution.py:430

commit v5 on v4

--- a/solution.py
+++ b/solution.py
@@ -39,6 +39,7 @@
     first_sem,
     first_pair_sem,
     bulk_sem,
+    direct_sem,
     x_sent,
     up_sent,
     down_sent,
@@ -47,6 +48,7 @@
     first_up_sent,
     first_pair_sent,
     bulk_sent,
+    direct_sent,
     local_sem,
     small_sem,
     up_here,
@@ -68,6 +70,10 @@
     usual, absent = no(corner), no(first)
     above = both(z == 1, x == 0)
     row = both(z == 0, x > 0)
+    near_row = both(z == 0, jnp.logical_or(x == 1, x == nx - 1))
+    helper = jnp.logical_or(near_row, above)
+    to_corner = {"tp": tp - z * CORES - core, "seq": 0}
+    near = sorted({1, nx - 1})
     pair = {"tp": tp + 1 - 2 * core}
     down = {"tp": tp - CORES + jnp.where(both(above, core == 0), 1, 0)}
 
@@ -93,8 +99,7 @@
         for step in range(1, nx):
             signal(barrier, along_seq(step))
         pl.when(z < last)(lambda: signal(barrier, up(core)))
-        pl.when(both(row, core == 1))(lambda: signal(barrier, {"tp": tp - 1, "seq": 0}))
-        pl.when(both(above, core == 1))(lambda: signal(barrier, {"tp": tp - CORES - 1}))
+        pl.when(jnp.logical_or(helper, both(row, core == 1)))(lambda: signal(barrier, to_corner))
 
     @pl.when(stand_in)
     def _():
@@ -102,7 +107,7 @@
         for step in range(1, nx):
             signal(barrier, {"tp": tp - 1, "seq": step})
 
-    greetings = jnp.where(first, nx + 1, jnp.where(stand_in, 2 * (nx - 1), nx + jnp.where(z > 0, 1, 0)))
+    greetings = jnp.where(first, nx + 2 + len(near), jnp.where(stand_in, 2 * (nx - 1), nx + jnp.where(z > 0, 1, 0)))
     pl.semaphore_wait(barrier, greetings)
     pl.when(z > 0)(lambda: signal(up_here, down))
 
@@ -181,6 +186,10 @@
     @pl.when(first)
     def _():
         signal(first_here, pair)
+        for of_core in range(CORES):
+            signal(first_here, {"tp": tp + CORES + of_core})
+            for k in near:
+                signal(first_here, {"tp": tp + of_core, "seq": k})
         away = [(k, {"tp": tp + 1, "seq": k}) for k in kinds[1:]]
         for steps, device in [away[-1], (0, {"tp": tp + CORES + 1}), *away[:-1], (0, pair)]:
             for piece in range(len(pieces)):
@@ -235,7 +244,7 @@
             @pl.when(stand_in)
             def _():
                 arrive(0, hops, kind)
-                if first_is_here:
+                if first_is_here and kind != kinds[-1]:
                     to_first_one(0, hops, kind).start()
                     to_first_one(1, hops, kind).start()
 
@@ -253,18 +262,38 @@
 
     def to_first(piece):
         kind, layer = pieces[piece]
-        block = cache.at[kind, layer, pl.ds(pages, (last * CORES * nx - 1) * pages)]
+        block = cache.at[kind, layer, pl.ds(CORES * nx * pages, (last - 1) * CORES * nx * pages)]
         return remote(block, block, bulk_sent, bulk_sem, pair)
+
+    def direct(of_core, of_x, src=None):
+        plane = 0 if of_x else last
+        of_seq = of_x if of_x else kinds[-1]
+        block = cache.at[:, :, pl.ds(((plane * CORES + of_core) * nx + of_seq) * pages, pages)]
+        landed = direct_sem.at[of_core * nx + of_x]
+        return remote(block if src is None else src, block, direct_sent, landed, to_corner)
+
+    def help_row():
+        pl.semaphore_wait(first_here, 1)
+        for of_core in range(CORES):
+            for k in near:
+                pl.when(both(core == of_core, x == k))(
+                    lambda of_core=of_core, k=k: direct(of_core, k, kv.at[:, :, 0]).start()
+                )
+
+    def help_above():
+        pl.semaphore_wait(first_here, 1)
+        for of_core in range(CORES):
+            pl.when(core == of_core)(lambda of_core=of_core: direct(of_core, 0).start())
 
     order = arrival_order(chips, kinds)
     for kind in kinds[1:-1]:
         own(kind)
-    near = max(at for at, (hops, _) in enumerate(order) if hops < last)
+    middle = max(at for at, (hops, _) in enumerate(order) if hops < last)
     for at, (hops, kind) in enumerate(order):
-        passing(hops, kind, at > near)
+        passing(hops, kind, at > middle)
         if at == 0:
             own(kinds[-1])
-        if at == near:
+        if at == middle:
 
             @pl.when(stand_in)
             def _():
@@ -272,13 +301,18 @@
                 pl.semaphore_wait(first_here, 1)
                 for piece in range(len(pieces)):
                     to_first(piece).start()
+                for of_core, of_seq in [(of_core, k) for of_core in range(CORES) for k in kinds]:
+                    if of_seq not in near and (of_core, of_seq) != (0, 0):
+                        to_first_one(of_core, 0, of_seq).start()
                 for far, of_kind in order[:at]:
-                    if far == last:
+                    if far == last and of_kind != kinds[-1]:
                         to_first_one(0, far, of_kind).start()
                         to_first_one(1, far, of_kind).start()
 
         if at == len(order) - 3:
             pl.when(both(row, core == 1))(pass_first)
+            pl.when(near_row)(help_row)
+    pl.when(above)(help_above)
     for copy in small:
         copy.wait()
     pl.when(no(stand_in))(lambda: local.wait())
@@ -312,7 +346,8 @@
     pl.when(both(below, core == 1))(lambda: blocks(1, first_up_sent).wait_send())
     pl.when(both(usual, core == 1))(lambda: blocks(1, first_pair_sent).wait_send())
     pl.when(both(usual, core == 0))(lambda: blocks(1, first_pair_sem).wait_recv())
-    handed = chips * CORES * nx - 1
+    handed = chips * CORES * nx - 1 - CORES * (len(near) + 1)
+    pl.when(helper)(lambda: blocks(1, direct_sent).wait_send())
 
     @pl.when(stand_in)
     def _():
@@ -323,6 +358,9 @@
     def _():
         blocks(nx + 1, first_sent).wait_send()
         blocks(handed, bulk_sem).wait_recv()
+        for of_core in range(CORES):
+            for of_x in [0, *near]:
+                direct(of_core, of_x).wait_recv()
 
 
 def attend(length, queries, cache, fresh):
@@ -360,7 +398,10 @@
         pltpu.make_async_copy(cache.at[:, :, page], place(page), sem).start()
         return 0
 
-    lax.fori_loop(1, pages, put, 0, unroll=15)
+    looped = 135
+    lax.fori_loop(1, looped + 1, put, 0, unroll=15)
+    for step in range(looped + 1, pages):
+        put(step, 0)
 
     def fresh(kind, layer):
         block = new_kv[kind, layer, 0].astype(jnp.float32)
@@ -411,10 +452,12 @@
             dma((pieces,)),
             dma,
             dma,
+            dma((CORES * nx,)),
             dma,
             dma((chips,)),
             dma((chips,)),
             dma((chips,)),
+            dma,
             dma,
             dma,
             dma,

time: 54 us -> 52.9 us (0.980)
  Pallas kernels: 52.6 us -> 51.1 us
    pallas_call x1, Pallas kernels: 49.4 us -> 48.3 us  [body(): pl.pallas_call(spread_kernel, out_shape=(pltpu.VMEM(cache_shape, kv_prefi...]
where the time goes in v5:
time: 52.9 us; the launch traced here: 52.4 us
  Pallas kernels  51.1 us (97%)
  between operations  1.29 us (2%)
    pallas_call x1, Pallas kernels, body(): pl.pallas_call(spread_kernel, out_shape=(pltpu.VMEM(cache_shape, kv_prefi...  48.3 us
    pallas_call x1, Pallas kernels, body(): pl.pallas_call(page_kernel, out_shape=(jax.ShapeDtypeStruct((kinds, layer...  2.75 us

profile of v5, /device:TPU:33, one launch (start us, length us, event | category | flops | bytes accessed | tf_op | source)
XLA Modules:
  0.0 52.4 jit_solution(7862684255113478821)
XLA Ops:
  1.3 48.3 %spread.1 = (bf16[2,2,256,16,128]{4,3,2,1,0:T(8,128)(2,1)S(1)}, s32[1,256]{1,0:T(1,128)S(4)}, bf16[2,128]{1,0:T(2,128)(2,1)S(1)}, bf16[2,2,1,8,128]{4,3,2,1,0:T(8,128)(2,1)S(1)}) custom-call(bf16[2,2,4,8,16,128]{5,4,3,2,1,0:T(8,128)(2,1)} %bitcast.3, s32[1,256]{1,0:T(1,128)} %slots.1, bf16[2,128]{1,0:T(2,128)(2,1)} %bitcast.4, bf16[2,2,1,8,128]{4,3,2,1,0:T(8,128)(2,1)} %new_kv.1), custom_call_target="tpu_custom_call" | custom-call | tf_op jit(solution)/shard_map/spread/pallas_call | solution.py:439
  49.6 2.7 %pages.1 = (bf16[2,2,1,256,16,128]{5,4,3,2,1,0:T(8,128)(2,1)}, bf16[2,128]{1,0:T(2,128)(2,1)}) custom-call(s32[1]{0:T(128)S(6)} %copy.7.lengths, s32[1,256]{1,0:T(1,128)S(4)} %get-tuple-element.8.slots, bf16[2,2,256,16,128]{4,3,2,1,0:T(8,128)(2,1)S(1)} %get-tuple-element.9.cache, bf16[2,128]{1,0:T(2,128)(2,1)S(1)} %get-tuple-element.10.queries, ...), custom_call_target="tpu_custom_call" | custom-call | tf_op jit(solution)/shard_map/pages/pallas_call | solution.py:473

commit v6 on v5

--- a/solution.py
+++ b/solution.py
@@ -40,6 +40,7 @@
     first_pair_sem,
     bulk_sem,
     direct_sem,
+    relay_sem,
     x_sent,
     up_sent,
     down_sent,
@@ -49,10 +50,12 @@
     first_pair_sent,
     bulk_sent,
     direct_sent,
+    relay_sent,
     local_sem,
     small_sem,
     up_here,
     first_here,
+    relayed,
 ):
     tp, x = lax.axis_index("tp"), lax.axis_index("seq")
     ranks, nx = lax.axis_size("tp"), lax.axis_size("seq")
@@ -70,10 +73,10 @@
     usual, absent = no(corner), no(first)
     above = both(z == 1, x == 0)
     row = both(z == 0, x > 0)
-    near_row = both(z == 0, jnp.logical_or(x == 1, x == nx - 1))
-    helper = jnp.logical_or(near_row, above)
+    helper = jnp.logical_or(row, above)
     to_corner = {"tp": tp - z * CORES - core, "seq": 0}
-    near = sorted({1, nx - 1})
+    others = range(1, nx)
+    relays = both(both(z == 0, x == nx - 1), core == 1)
     pair = {"tp": tp + 1 - 2 * core}
     down = {"tp": tp - CORES + jnp.where(both(above, core == 0), 1, 0)}
 
@@ -99,7 +102,7 @@
         for step in range(1, nx):
             signal(barrier, along_seq(step))
         pl.when(z < last)(lambda: signal(barrier, up(core)))
-        pl.when(jnp.logical_or(helper, both(row, core == 1)))(lambda: signal(barrier, to_corner))
+        pl.when(helper)(lambda: signal(barrier, to_corner))
 
     @pl.when(stand_in)
     def _():
@@ -107,7 +110,7 @@
         for step in range(1, nx):
             signal(barrier, {"tp": tp - 1, "seq": step})
 
-    greetings = jnp.where(first, nx + 2 + len(near), jnp.where(stand_in, 2 * (nx - 1), nx + jnp.where(z > 0, 1, 0)))
+    greetings = jnp.where(first, 2 * nx + 1, jnp.where(stand_in, 2 * (nx - 1), nx + jnp.where(z > 0, 1, 0)))
     pl.semaphore_wait(barrier, greetings)
     pl.when(z > 0)(lambda: signal(up_here, down))
 
@@ -157,6 +160,8 @@
             along_seq(-kind),
         )
 
+    kinds = [0, *sorted(range(1, nx), key=lambda k: (min(k, nx - k), k))]
+
     def first_piece(piece):
         kind, layer = pieces[piece]
         start = start_of(0, 0, lax.rem(nx - x, nx))
@@ -172,6 +177,23 @@
             device,
         )
 
+    half, far = len(pieces) // 2, kinds[-1]
+
+    def first_relay(at):
+        kind, layer = pieces[half + at]
+        by = {"tp": tp + 1, "seq": nx - 1}
+        return remote(kv.at[kind, layer, far], relayed.at[at], first_sent, relay_sem.at[at], by)
+
+    def relay_on(at):
+        kind, layer = pieces[half + at]
+        block = cache.at[kind, layer, pl.ds(0, pages)]
+        return remote(relayed.at[at], block, relay_sent, first_sem.at[half + at], {"seq": far})
+
+    def relay():
+        for at in range(half):
+            first_relay(at).wait_recv()
+            relay_on(at).start()
+
     def first_up(piece):
         block = first_piece(piece)
         return remote(block, block, first_up_sent, first_sem.at[piece], up(core))
@@ -180,7 +202,6 @@
         block = first_piece(piece)
         return remote(block, block, first_pair_sent, first_pair_sem, pair)
 
-    kinds = [0, *sorted(range(1, nx), key=lambda k: (min(k, nx - k), k))]
     mine = kv.at[:, :, x]
 
     @pl.when(first)
@@ -188,12 +209,17 @@
         signal(first_here, pair)
         for of_core in range(CORES):
             signal(first_here, {"tp": tp + CORES + of_core})
-            for k in near:
+            for k in others:
                 signal(first_here, {"tp": tp + of_core, "seq": k})
-        away = [(k, {"tp": tp + 1, "seq": k}) for k in kinds[1:]]
-        for steps, device in [away[-1], (0, {"tp": tp + CORES + 1}), *away[:-1], (0, pair)]:
-            for piece in range(len(pieces)):
-                first_to(steps, piece, device).start()
+        every = range(len(pieces))
+        sends = [(k, piece) for piece in every[:half] for k in (far, *kinds[1:-1], 0)]
+        sends += [(k, piece) for piece in every[half:] for k in (*kinds[1:-1], 0)]
+        for at in range(half):
+            first_relay(at).start()
+        for k, piece in sends:
+            first_to(k, piece, {"tp": tp + (1 if k else CORES + 1), "seq": k}).start()
+        for piece in every:
+            first_to(0, piece, pair).start()
 
     pl.when(z > 0)(lambda: to_down(z, 0, mine).start())
 
@@ -275,7 +301,7 @@
     def help_row():
         pl.semaphore_wait(first_here, 1)
         for of_core in range(CORES):
-            for k in near:
+            for k in others:
                 pl.when(both(core == of_core, x == k))(
                     lambda of_core=of_core, k=k: direct(of_core, k, kv.at[:, :, 0]).start()
                 )
@@ -301,17 +327,16 @@
                 pl.semaphore_wait(first_here, 1)
                 for piece in range(len(pieces)):
                     to_first(piece).start()
-                for of_core, of_seq in [(of_core, k) for of_core in range(CORES) for k in kinds]:
-                    if of_seq not in near and (of_core, of_seq) != (0, 0):
-                        to_first_one(of_core, 0, of_seq).start()
+                to_first_one(1, 0, 0).start()
                 for far, of_kind in order[:at]:
                     if far == last and of_kind != kinds[-1]:
                         to_first_one(0, far, of_kind).start()
                         to_first_one(1, far, of_kind).start()
 
         if at == len(order) - 3:
+            pl.when(row)(help_row)
+            pl.when(relays)(relay)
             pl.when(both(row, core == 1))(pass_first)
-            pl.when(near_row)(help_row)
     pl.when(above)(help_above)
     for copy in small:
         copy.wait()
@@ -346,8 +371,9 @@
     pl.when(both(below, core == 1))(lambda: blocks(1, first_up_sent).wait_send())
     pl.when(both(usual, core == 1))(lambda: blocks(1, first_pair_sent).wait_send())
     pl.when(both(usual, core == 0))(lambda: blocks(1, first_pair_sem).wait_recv())
-    handed = chips * CORES * nx - 1 - CORES * (len(near) + 1)
+    handed = chips * CORES * nx - 1 - CORES * nx
     pl.when(helper)(lambda: blocks(1, direct_sent).wait_send())
+    pl.when(relays)(lambda: remote(relayed, relayed, relay_sent, relay_sent, pair).wait_send())
 
     @pl.when(stand_in)
     def _():
@@ -359,7 +385,7 @@
         blocks(nx + 1, first_sent).wait_send()
         blocks(handed, bulk_sem).wait_recv()
         for of_core in range(CORES):
-            for of_x in [0, *near]:
+            for of_x in range(nx):
                 direct(of_core, of_x).wait_recv()
 
 
@@ -453,6 +479,7 @@
             dma,
             dma,
             dma((CORES * nx,)),
+            dma((pieces // 2,)),
             dma,
             dma((chips,)),
             dma((chips,)),
@@ -463,9 +490,11 @@
             dma,
             dma,
             dma,
+            dma,
             dma((3,)),
             pltpu.SemaphoreType.REGULAR,
             pltpu.SemaphoreType.REGULAR,
+            pltpu.VMEM((pieces // 2, positions // PAGE, PAGE, head), kv_prefill.dtype),
         ],
         compiler_params=pltpu.CompilerParams(collective_id=0, has_side_effects=True, vmem_limit_bytes=16 * MIB),
         name="spread",

time: 52.9 us -> 52.3 us (0.989)
  no operation moved by 1% of the time
where the time goes in v6:
time: 52.3 us; the launch traced here: 52 us
  Pallas kernels  50.7 us (97%)
  between operations  1.29 us (2%)
    pallas_call x1, Pallas kernels, body(): pl.pallas_call(spread_kernel, out_shape=(pltpu.VMEM(cache_shape, kv_prefi...  48 us
    pallas_call x1, Pallas kernels, body(): pl.pallas_call(page_kernel, out_shape=(jax.ShapeDtypeStruct((kinds, layer...  2.75 us

profile of v6, /device:TPU:33, one launch (start us, length us, event | category | flops | bytes accessed | tf_op | source)
XLA Modules:
  0.0 52.0 jit_solution(5550422735813574471)
XLA Ops:
  1.3 48.0 %spread.1 = (bf16[2,2,256,16,128]{4,3,2,1,0:T(8,128)(2,1)S(1)}, s32[1,256]{1,0:T(1,128)S(4)}, bf16[2,128]{1,0:T(2,128)(2,1)S(1)}, bf16[2,2,1,8,128]{4,3,2,1,0:T(8,128)(2,1)S(1)}) custom-call(bf16[2,2,4,8,16,128]{5,4,3,2,1,0:T(8,128)(2,1)} %bitcast.3, s32[1,256]{1,0:T(1,128)} %slots.1, bf16[2,128]{1,0:T(2,128)(2,1)} %bitcast.4, bf16[2,2,1,8,128]{4,3,2,1,0:T(8,128)(2,1)} %new_kv.1), custom_call_target="tpu_custom_call" | custom-call | tf_op jit(solution)/shard_map/spread/pallas_call | solution.py:465
  49.3 2.7 %pages.1 = (bf16[2,2,1,256,16,128]{5,4,3,2,1,0:T(8,128)(2,1)}, bf16[2,128]{1,0:T(2,128)(2,1)}) custom-call(s32[1]{0:T(128)S(6)} %copy.7.lengths, s32[1,256]{1,0:T(1,128)S(4)} %get-tuple-element.8.slots, bf16[2,2,256,16,128]{4,3,2,1,0:T(8,128)(2,1)S(1)} %get-tuple-element.9.cache, bf16[2,128]{1,0:T(2,128)(2,1)S(1)} %get-tuple-element.10.queries, ...), custom_call_target="tpu_custom_call" | custom-call | tf_op jit(solution)/shard_map/pages/pallas_call | solution.py:502
